TPU v7x, 32 devices: a whole 2x2x4 slice. The times are simulated.
32 devices in a mesh: dp: 8 (over z, x), ep: 4 (over y, core).
Axes of the slice: x: 2, y: 2, z: 4, core: 2. Of those that a mesh axis runs over, the one named last changes fastest.
Arguments:
- tokens: bfloat16 [64, 197, 768], P(('dp', 'ep')), may hold values from -6 to 6
- live_images: int32 [32], P(('dp', 'ep')), may hold values from 1 to 2, as said below
- routes: int32 [64, 197, 2], P(('dp', 'ep')), may hold values from 0 to 3, all different within a row; in each aligned block of 394 rows (0 to 393, 394 to 787, ..., all dimensions but the last counted through in order) at most 248 rows name the same one
- ln1_gain: float32 [768], replicated, may hold values from 0.1 to 1.9
- ln1_bias: float32 [768], replicated, may hold values from -3 to 3
- query_key_value_weight: bfloat16 [768, 2304], replicated, may hold values from -0.21875 to 0.21875
- attention_output_weight: bfloat16 [768, 768], replicated, may hold values from -0.625 to 0.625
- ln2_gain: float32 [768], replicated, may hold values from 0.1 to 1.9
- ln2_bias: float32 [768], replicated, may hold values from -3 to 3
- w_router: bfloat16 [768, 4], replicated, may hold values from -0.4375 to 0.4375
- w_in: bfloat16 [4, 768, 3072], P('ep'), may hold values from -0.21875 to 0.21875
- w_out: bfloat16 [4, 3072, 768], P('ep'), may hold values from -0.875 to 0.875
- cotangent: bfloat16 [64, 197, 768], P(('dp', 'ep')), may hold values from -6 to 6
Outputs:
- block_out: bfloat16 [64, 197, 768], P(('dp', 'ep'))
- grad_tokens: float32 [64, 197, 768], P(('dp', 'ep'))
- grad_ln1_gain: float32 [768], P('ep')
- grad_ln1_bias: float32 [768], P('ep')
- grad_w_qkv: float32 [768, 2304], P('ep')
- grad_w_attn_out: float32 [768, 768], P('ep')
- grad_ln2_gain: float32 [768], P('ep')
- grad_ln2_bias: float32 [768], P('ep')
- grad_w_router: float32 [768, 4], P('ep')
- grad_w_in: float32 [4, 768, 3072], P('ep', 'dp')
- grad_w_out: float32 [4, 3072, 768], P('ep', 'dp')
Inputs may be any that keep to these rules, and one draw needn't show every extreme that they name: Each device holds 2 image slots of which the first live_images are images; some device holds 2, some holds one. `routes`: each token names two different experts. Among the 394 tokens of one device, slots live or not, no expert is named more than 248 times, a bound that some block reaches.
All inputs are finite; a program needn't handle non-finite values.
Results may differ from a plain program's by a relative error of at most 0.024.
Values may be sent and summed in bfloat16 or wider, within the bound.
A program may use at most 192 MiB of HBM per device.

v0:
```python
import jax
import jax.numpy as jnp
from jax import lax
from jax.sharding import PartitionSpec as P

HEADS = 12
HEAD_DIM = 64


eps = 1e-06


def norm_forward(values):
    centre = jnp.mean(values, axis=-1, keepdims=True)
    shifted = values - centre
    inverse = lax.rsqrt(jnp.mean(shifted * shifted, axis=-1, keepdims=True) + eps)
    return (shifted * inverse, inverse)


def norm_backward(grad_normed, normalized_input, inverse):
    middle = jnp.mean(grad_normed, axis=-1, keepdims=True)
    along = jnp.mean(grad_normed * normalized_input, axis=-1, keepdims=True)
    return (grad_normed - middle - normalized_input * along) * inverse


def body(
    tokens,
    live_images,
    routes,
    ln1_gain,
    ln1_bias,
    query_key_value_weight,
    attention_output_weight,
    ln2_gain,
    ln2_bias,
    w_router,
    w_in,
    w_out,
    cotangent,
):
    slot_count, seq_len, model_width = tokens.shape
    row_count = slot_count * seq_len
    expert_count = w_router.shape[1]
    hidden_width = w_in.shape[2]
    capacity = ((2 * row_count + expert_count - 1) // expert_count * 5 // 4 + 7) // 8 * 8
    scaling = HEAD_DIM ** (-0.5)
    inputs = tokens.astype(jnp.float32).reshape(row_count, model_width)
    normed1, inverse1 = norm_forward(inputs)
    attn_in = (normed1 * ln1_gain + ln1_bias).astype(jnp.bfloat16)
    qkv_rows = jnp.dot(attn_in, query_key_value_weight, preferred_element_type=jnp.float32).astype(
        jnp.bfloat16
    )
    qkv_heads = qkv_rows.reshape(slot_count, seq_len, 3, HEADS, HEAD_DIM)
    queries = qkv_heads[:, :, 0]
    keys_all = qkv_heads[:, :, 1]
    values_all = qkv_heads[:, :, 2]
    scores = (
        jnp.einsum("sqhc,skhc->shqk", queries, keys_all, preferred_element_type=jnp.float32)
        * scaling
    )
    row_peak = jnp.max(scores, axis=-1, keepdims=True)
    raised = jnp.exp(scores - row_peak)
    totals = jnp.sum(raised, axis=-1, keepdims=True)
    log_total = row_peak + jnp.log(totals)
    weights = (raised / totals).astype(jnp.bfloat16)
    attended_context = jnp.einsum(
        "shqk,skhc->sqhc", weights, values_all, preferred_element_type=jnp.float32
    )
    attended_context = attended_context.astype(jnp.bfloat16).reshape(row_count, model_width)
    hidden1 = inputs + jnp.dot(
        attended_context, attention_output_weight, preferred_element_type=jnp.float32
    )
    normed2, inverse2 = norm_forward(hidden1)
    moe_in = (normed2 * ln2_gain + ln2_bias).astype(jnp.bfloat16)
    router = jax.nn.softmax(jnp.dot(moe_in, w_router, preferred_element_type=jnp.float32), axis=-1)
    chosen = routes.reshape(row_count, 2)
    expert_ids = jnp.arange(expert_count, dtype=jnp.int32)
    picked = (chosen[:, :, None] == expert_ids[None, None, :]).astype(jnp.float32)
    gates = jnp.sum(picked * router[:, None, :], axis=-1)
    token_live = (jnp.arange(row_count, dtype=jnp.int32) // seq_len < live_images[0]).astype(
        jnp.float32
    )
    pair_ids = chosen.reshape(2 * row_count)
    pair_live = jnp.repeat(token_live, 2) > 0.5
    member = ((pair_ids[:, None] == expert_ids[None, :]) & pair_live[:, None]).astype(jnp.int32)
    position = jnp.sum((jnp.cumsum(member, axis=0) - 1) * member, axis=-1)
    slot_ids = jnp.where(pair_live, pair_ids * capacity + position, -1).reshape(row_count, 2)
    lanes = jnp.arange(expert_count * capacity, dtype=jnp.int32)
    placing = (jnp.transpose(slot_ids)[:, None, :] == lanes[None, :, None]).astype(jnp.bfloat16)
    outbox = jnp.einsum("jsr,rd->sd", placing, moe_in, preferred_element_type=jnp.float32)
    outbox = outbox.astype(jnp.bfloat16).reshape(expert_count, capacity, model_width)
    inbox = lax.all_to_all(outbox, "ep", split_axis=0, concat_axis=0, tiled=True)
    flat_in = inbox.reshape(-1, model_width)
    pre_act = jnp.dot(flat_in, w_in[0], preferred_element_type=jnp.float32)
    activated = jax.nn.gelu(pre_act).astype(jnp.bfloat16)
    produced = jnp.dot(activated, w_out[0], preferred_element_type=jnp.float32).astype(jnp.bfloat16)
    coming_back = lax.all_to_all(
        produced.reshape(inbox.shape), "ep", split_axis=0, concat_axis=0, tiled=True
    )
    coming_back, pre_act = (
        coming_back,
        pre_act.reshape(inbox.shape[0], inbox.shape[1], hidden_width),
    )
    arrived_rows = inbox.reshape(-1, model_width)
    pre_rows = pre_act.reshape(-1, hidden_width)
    returned_rows = coming_back.reshape(expert_count * capacity, model_width)
    taken = jnp.einsum("jsr,sd->rjd", placing, returned_rows, preferred_element_type=jnp.float32)
    mixture = jnp.sum(gates[:, :, None] * taken, axis=1)
    block_out = (
        ((hidden1 + mixture) * token_live[:, None]).astype(jnp.bfloat16).reshape(tokens.shape)
    )
    upstream = cotangent.astype(jnp.float32).reshape(row_count, model_width) * token_live[:, None]
    gate_grads = jnp.sum(taken * upstream[:, None, :], axis=-1)
    sent_grads = (gates[:, :, None] * upstream[:, None, :]).astype(jnp.bfloat16)
    grad_outbox = jnp.einsum("jsr,rjd->sd", placing, sent_grads, preferred_element_type=jnp.float32)
    grad_outbox = grad_outbox.astype(jnp.bfloat16).reshape(expert_count, capacity, model_width)
    grad_inbox = lax.all_to_all(grad_outbox, "ep", split_axis=0, concat_axis=0, tiled=True)
    grad_rows = grad_inbox.reshape(-1, model_width)
    activated_rows, gelu_pull = jax.vjp(jax.nn.gelu, pre_rows)
    activated_low = activated_rows.astype(jnp.bfloat16)
    grad_activated = jnp.einsum(
        "rd,fd->rf", grad_rows, w_out[0], preferred_element_type=jnp.float32
    )
    grad_pre = gelu_pull(grad_activated)[0].astype(jnp.bfloat16)
    columns = activated_low
    grad_w_out = lax.psum_scatter(
        jnp.einsum("rf,rd->fd", columns, grad_rows, preferred_element_type=jnp.float32).astype(
            jnp.bfloat16
        ),
        "dp",
        scatter_dimension=0,
        tiled=True,
    ).astype(jnp.float32)
    grad_back_rows = jnp.einsum(
        "rf,df->rd", grad_pre, w_in[0], preferred_element_type=jnp.float32
    ).astype(jnp.bfloat16)
    grad_back = lax.all_to_all(
        grad_back_rows.reshape(grad_inbox.shape), "ep", split_axis=0, concat_axis=0, tiled=True
    )
    columns = arrived_rows
    grad_w_in = lax.psum_scatter(
        jnp.einsum("rd,rf->df", columns, grad_pre, preferred_element_type=jnp.float32).astype(
            jnp.bfloat16
        ),
        "dp",
        scatter_dimension=0,
        tiled=True,
    ).astype(jnp.float32)
    grad_back_flat = grad_back.reshape(expert_count * capacity, model_width)
    expert_grad = jnp.einsum(
        "jsr,sd->rd", placing, grad_back_flat, preferred_element_type=jnp.float32
    )
    grad_router_probs = jnp.sum(gate_grads[:, :, None] * picked, axis=1)
    grad_logits = router * (
        grad_router_probs - jnp.sum(router * grad_router_probs, axis=-1, keepdims=True)
    )
    grad_logits = grad_logits.astype(jnp.bfloat16)
    grad_w_router = jnp.einsum("rd,re->de", moe_in, grad_logits, preferred_element_type=jnp.float32)
    grad_moe_in = expert_grad + jnp.einsum(
        "re,de->rd", grad_logits, w_router, preferred_element_type=jnp.float32
    )
    grad_ln2_gain = jnp.sum(grad_moe_in * normed2, axis=0)
    grad_ln2_bias = jnp.sum(grad_moe_in, axis=0)
    grad_hidden1 = upstream + norm_backward(grad_moe_in * ln2_gain, normed2, inverse2)
    grad_attn = grad_hidden1.astype(jnp.bfloat16)
    grad_w_attn_out = jnp.einsum(
        "rd,re->de", attended_context, grad_attn, preferred_element_type=jnp.float32
    )
    grad_context = jnp.einsum(
        "re,de->rd", grad_attn, attention_output_weight, preferred_element_type=jnp.float32
    )
    grad_context = grad_context.astype(jnp.bfloat16).reshape(slot_count, seq_len, HEADS, HEAD_DIM)
    again = (
        jnp.einsum("sqhc,skhc->shqk", queries, keys_all, preferred_element_type=jnp.float32)
        * scaling
    )
    probs_again = jnp.exp(again - log_total)
    probs_low = probs_again.astype(jnp.bfloat16)
    grad_values = jnp.einsum(
        "shqk,sqhc->skhc", probs_low, grad_context, preferred_element_type=jnp.float32
    )
    grad_probs = jnp.einsum(
        "sqhc,skhc->shqk", grad_context, values_all, preferred_element_type=jnp.float32
    )
    grad_scores = probs_again * (
        grad_probs - jnp.sum(probs_again * grad_probs, axis=-1, keepdims=True)
    )
    grad_scores = grad_scores.astype(jnp.bfloat16)
    grad_queries = (
        jnp.einsum("shqk,skhc->sqhc", grad_scores, keys_all, preferred_element_type=jnp.float32)
        * scaling
    )
    grad_keys = (
        jnp.einsum("shqk,sqhc->skhc", grad_scores, queries, preferred_element_type=jnp.float32)
        * scaling
    )
    grad_qkv = (
        jnp.stack([grad_queries, grad_keys, grad_values], axis=2)
        .astype(jnp.bfloat16)
        .reshape(row_count, 3 * model_width)
    )
    grad_w_qkv = jnp.einsum("rd,re->de", attn_in, grad_qkv, preferred_element_type=jnp.float32)
    grad_attn_in = jnp.einsum(
        "re,de->rd", grad_qkv, query_key_value_weight, preferred_element_type=jnp.float32
    )
    grad_ln1_gain = jnp.sum(grad_attn_in * normed1, axis=0)
    grad_ln1_bias = jnp.sum(grad_attn_in, axis=0)
    grad_inputs = grad_hidden1 + norm_backward(grad_attn_in * ln1_gain, normed1, inverse1)
    shared = (
        grad_w_qkv,
        grad_w_attn_out,
        grad_w_router,
        grad_ln1_gain,
        grad_ln1_bias,
        grad_ln2_gain,
        grad_ln2_bias,
    )
    partial_sums = (
        lax.psum_scatter(
            shared[0].astype(jnp.bfloat16), "ep", scatter_dimension=0, tiled=True
        ).astype(jnp.float32),
        lax.psum_scatter(
            shared[1].astype(jnp.bfloat16), "ep", scatter_dimension=0, tiled=True
        ).astype(jnp.float32),
        lax.psum_scatter(
            shared[2].astype(jnp.bfloat16), "ep", scatter_dimension=0, tiled=True
        ).astype(jnp.float32),
        lax.psum_scatter(
            shared[3].astype(jnp.bfloat16), "ep", scatter_dimension=0, tiled=True
        ).astype(jnp.float32),
        lax.psum_scatter(
            shared[4].astype(jnp.bfloat16), "ep", scatter_dimension=0, tiled=True
        ).astype(jnp.float32),
        lax.psum_scatter(
            shared[5].astype(jnp.bfloat16), "ep", scatter_dimension=0, tiled=True
        ).astype(jnp.float32),
        lax.psum_scatter(
            shared[6].astype(jnp.bfloat16), "ep", scatter_dimension=0, tiled=True
        ).astype(jnp.float32),
    )
    shares = (
        lax.psum(partial_sums[0].astype(jnp.bfloat16), "dp").astype(jnp.float32),
        lax.psum(partial_sums[1].astype(jnp.bfloat16), "dp").astype(jnp.float32),
        lax.psum(partial_sums[2].astype(jnp.bfloat16), "dp").astype(jnp.float32),
        lax.psum(partial_sums[3].astype(jnp.bfloat16), "dp").astype(jnp.float32),
        lax.psum(partial_sums[4].astype(jnp.bfloat16), "dp").astype(jnp.float32),
        lax.psum(partial_sums[5].astype(jnp.bfloat16), "dp").astype(jnp.float32),
        lax.psum(partial_sums[6].astype(jnp.bfloat16), "dp").astype(jnp.float32),
    )
    return (
        block_out,
        grad_inputs.reshape(tokens.shape),
        shares[3],
        shares[4],
        shares[0],
        shares[1],
        shares[5],
        shares[6],
        shares[2],
        grad_w_in[None],
        grad_w_out[None],
    )


def solution(mesh):
    in_specs = (
        P(("dp", "ep"), None, None),
        P(("dp", "ep")),
        P(("dp", "ep"), None, None),
        P(),
        P(),
        P(),
        P(),
        P(),
        P(),
        P(),
        P("ep", None, None),
        P("ep", None, None),
        P(("dp", "ep"), None, None),
    )
    out_specs = (
        P(("dp", "ep"), None, None),
        P(("dp", "ep"), None, None),
        P("ep"),
        P("ep"),
        P("ep", None),
        P("ep", None),
        P("ep"),
        P("ep"),
        P("ep", None),
        P("ep", "dp", None),
        P("ep", "dp", None),
    )
    return jax.shard_map(body, mesh=mesh, in_specs=in_specs, out_specs=out_specs, check_vma=False)
```

profile of v0, /device:TPU:0, one launch (start us, length us, event | category | flops | bytes accessed | tf_op | source)
XLA Modules:
  0.0 590.4 jit_solution(2008736721865741235)
XLA Ops:
  40.4 4.2 convolution_convert_fusion.3
  44.6 6.6 %reshape.268 = bf16[2,197,3,12,64]{4,3,2,1,0:T(8,128)(2,1)} reshape(bf16[394,2304]{1,0:T(8,128)(2,1)} %convolution_convert_fusion.3) | data formatting | bytes 3631104 | tf_op jit(solution)/shard_map/reshape | solution.py:53
  51.3 5.0 fusion.71
  83.4 4.4 all-to-all-start
  97.5 3.7 bitcast_convert_fusion
  101.2 6.8 %all-to-all-done = bf16[4,248,768]{2,1,0:T(8,128)(2,1)} async-done(((bf16[4,248,768]{2,1,0:T(8,128)(2,1)}), bf16[4,248,768]{2,1,0:T(8,128)(2,1)}, u32[]{:S(2)}, u32[]{:S(2)}) %all-to-all-start) | async-done | bytes 1523744 | tf_op jit(solution)/shard_map/all_to_all | solution.py:92
  108.0 4.4 all-to-all-start.2
  112.4 7.2 %fusion.13 = f32[992,3072]{1,0:T(8,128)S(1)} fusion(bf16[992,768]{1,0:T(8,128)(2,1)} %bitcast.8, bf16[1,768,3072]{2,1,0:T(8,128)(2,1)} %param.23), kind=kOutput, calls=%fused_computation.25 | convolution fusion | flops 4680843264 | bytes 18432000 | tf_op jit(solution)/shard_map/dot_general | solution.py:94
  119.6 4.4 copy-done.56
  124.0 10.6 %fusion.32 = bf16[992,768]{1,0:T(8,128)(2,1)} fusion(bf16[1,3072,768]{2,1,0:T(8,128)(2,1)} %param.24, f32[992,3072]{1,0:T(8,128)S(1)} %fusion.13), kind=kOutput, calls=%fused_computation.48 | convolution fusion | flops 4709031936 | bytes 18432000 | tf_op jit(solution)/shard_map/dot_general | solution.py:96
  134.5 4.6 all-to-all-start.1
  139.1 14.9 %fusion.6 = bf16[992,3072]{1,0:T(8,128)(2,1)S(1)} fusion(f32[992,3072]{1,0:T(8,128)} %copy-done.56, bf16[992,768]{1,0:T(8,128)(2,1)} %bitcast.17, bf16[1,3072,768]{2,1,0:T(8,128)(2,1)} %param.24), kind=kOutput, calls=%fused_computation.8 | convolution fusion | flops 4741791744 | bytes 24526848 | tf_op jit(solution)/shard_map/rd,fd->rf/dot_general | solution.py:121
  156.6 8.3 %fusion.29 = bf16[992,768]{1,0:T(8,128)(2,1)} fusion(bf16[992,3072]{1,0:T(8,128)(2,1)S(1)} %fusion.6, bf16[1,768,3072]{2,1,0:T(8,128)(2,1)} %param.23), kind=kOutput, calls=%fused_computation.47 | convolution fusion | flops 4681605120 | bytes 12337152 | tf_op jit(solution)/shard_map/rf,df->rd/dot_general | solution.py:134
  165.0 4.5 all-to-all-start.3
  176.0 4.7 fusion.25
  181.4 7.6 %all-to-all-done.3 = bf16[4,248,768]{2,1,0:T(8,128)(2,1)} async-done(((bf16[4,248,768]{2,1,0:T(8,128)(2,1)}), bf16[4,248,768]{2,1,0:T(8,128)(2,1)}, u32[]{:S(2)}, u32[]{:S(2)}) %all-to-all-start.3) | async-done | bytes 1523744 | tf_op jit(solution)/shard_map/all_to_all | solution.py:137
  200.8 3.5 reshape.269
  207.3 4.7 multiply_reduce_fusion
  212.0 3.6 multiply_convert_fusion.1
  219.5 3.9 copy.137
  223.3 6.7 %convert_element_type.186 = bf16[394,2304]{0,1:T(8,128)(2,1)} reshape(bf16[2,197,3,12,64]{1,0,4,3,2:T(2,128)(2,1)} %copy.137) | data formatting | bytes 3631104 | tf_op jit(solution)/shard_map/convert_element_type | solution.py:199
  230.0 5.8 convolution_convert_fusion.2
  239.4 38.2 %reduce-scatter.8.cloned.1.call-done = bf16[192,2304]{1,0:T(8,128)(2,1)} async-done(((bf16[768,2304]{1,0:T(8,128)(2,1)}), bf16[192,2304]{1,0:T(8,128)(2,1)}) %reduce-scatter.8.cloned.1.call-update) | async-done | bytes 884752 | tf_op jit(solution)/shard_map/reduce_scatter | solution.py:219
  277.6 11.8 %convolution_convert_fusion = bf16[3072,768]{1,0:T(8,128)(2,1)} fusion(bf16[992,768]{1,0:T(8,128)(2,1)} %bitcast.17, f32[992,3072]{1,0:T(8,128)} %copy-done.56), kind=kOutput, calls=%fused_computation.10 | convolution fusion | flops 4710629376 | bytes 18432000 | tf_op jit(solution)/shard_map/rf,rd->fd/dot_general | solution.py:127
  289.5 9.1 %convolution_convert_fusion.1 = bf16[768,3072]{1,0:T(8,128)(2,1)} fusion(bf16[992,768]{1,0:T(8,128)(2,1)} %bitcast.8, bf16[992,3072]{1,0:T(8,128)(2,1)} %copy-done.55), kind=kOutput, calls=%fused_computation.11 | convolution fusion | flops 4683202560 | bytes 12337152 | tf_op jit(solution)/shard_map/rd,rf->df/dot_general | solution.py:142
  304.9 5.9 multiply_reduce_fusion.3
  310.8 6.8 %all-reduce.7 = (bf16[768]{0:T(1024)(128)(2,1)}, bf16[768]{0:T(1024)(128)(2,1)}, bf16[768]{0:T(1024)(128)(2,1)}, bf16[768]{0:T(1024)(128)(2,1)}) all-reduce(bf16[768]{0:T(1024)(128)(2,1)} %get-tuple-element.68, bf16[768]{0:T(1024)(128)(2,1)} %get-tuple-element.75, ...), channel_id=2, replica_groups=mesh['dp'=8,'ep'=4] {'ep'}, use_global_device_ids=true, to_apply=%region_23.24.clone | all-reduce | flops 3072 | bytes 12288
  323.5 3.5 multiply_add_fusion
  333.4 22.1 %all-reduce.5 = (bf16[192]{0:T(256)(128)(2,1)}, bf16[192]{0:T(256)(128)(2,1)}, bf16[192]{0:T(256)(128)(2,1)}, bf16[192]{0:T(256)(128)(2,1)}, bf16[192,4]{0,1:T(4,128)(2,1)S(1)}) all-reduce(bf16[192]{0:T(256)(128)(2,1)S(1)} %dynamic-slice.1, bf16[192]{0:T(256)(128)(2,1)S(1)} %copy-done.53, ...), channel_id=1, replica_groups=mesh['dp'=8,'ep'=4] {'dp'}, use_global_device_ids=true, to_apply=%region_24.25 | all-reduce | flops 1536 | bytes 6144 | tf_op jit(solution)/shard_map/psum | solution.py:245
  360.9 23.1 %all-reduce.10.cloned.1.call-done = (bf16[192,2304]{1,0:T(8,128)(2,1)}, bf16[192,768]{1,0:T(8,128)(2,1)}) async-done(((bf16[192,2304]{1,0:T(8,128)(2,1)}, bf16[192,768]{1,0:T(8,128)(2,1)}), (bf16[192,2304]{1,0:T(8,128)(2,1)}, bf16[192,768]{1,0:T(8,128)(2,1)})) %all-reduce.10.cloned.1.call-update) | async-done | bytes 1179664 | tf_op jit(solution)/shard_map/psum | solution.py:242
  388.4 94.0 %reduce-scatter.14.cloned.1.call-done = bf16[384,768]{1,0:T(8,128)(2,1)} async-done(((bf16[3072,768]{1,0:T(8,128)(2,1)}), bf16[384,768]{1,0:T(8,128)(2,1)}) %reduce-scatter.14.cloned.1.call-update) | async-done | bytes 589840 | tf_op jit(solution)/shard_map/reduce_scatter | solution.py:126
  484.5 96.7 %reduce-scatter.12.cloned.1.call-done = bf16[96,3072]{1,0:T(8,128)(2,1)} async-done(((bf16[768,3072]{1,0:T(8,128)(2,1)}), bf16[96,3072]{1,0:T(8,128)(2,1)}) %reduce-scatter.12.cloned.1.call-update) | async-done | bytes 589840 | tf_op jit(solution)/shard_map/reduce_scatter | solution.py:141
  (226 shorter events, 132.9 us)
Async XLA Ops:
  7.2 33.2 %copy-start = (bf16[768,2304]{1,0:T(8,128)(2,1)S(1)}, bf16[768,2304]{1,0:T(8,128)(2,1)}, u32[]{:S(2)}) copy-start(bf16[768,2304]{1,0:T(8,128)(2,1)} %param.18) | copy-start | bytes 10616836
  20.9 5.0 copy-start.42
  32.7 7.6 %copy-start.39 = (f32[768]{0:T(1024)S(1)}, f32[768]{0:T(1024)}, u32[]{:S(2)}) copy-start(f32[768]{0:T(1024)} %param.16) | copy-start | bytes 9220
  32.7 7.6 %copy-start.43 = (f32[394]{0:T(512)S(1)}, f32[394]{0:T(512)}, u32[]{:S(2)}) copy-start(f32[394]{0:T(512)} %div.53) | copy-start | bytes 4732
  32.8 7.6 %copy-start.45 = (f32[394]{0:T(512)S(1)}, f32[394]{0:T(512)}, u32[]{:S(2)}) copy-start(f32[394]{0:T(512)} %rsqrt.21) | copy-start | bytes 4732
  83.4 24.6 %all-to-all-start = ((bf16[4,248,768]{2,1,0:T(8,128)(2,1)}), bf16[4,248,768]{2,1,0:T(8,128)(2,1)}, u32[]{:S(2)}, u32[]{:S(2)}) async-start(bf16[4,248,768]{2,1,0:T(8,128)(2,1)} %bitcast.131), calls=%async_computation | async-start | bytes 3047424 | tf_op jit(solution)/shard_map/all_to_all | solution.py:92
  87.8 7.2 %copy-start.21 = (s32[394,2]{0,1:T(2,128)S(1)}, s32[394,2]{0,1:T(2,128)}, u32[]{:S(2)}) copy-start(s32[394,2]{0,1:T(2,128)} %eq.50) | copy-start | bytes 9460
  89.2 7.3 %copy-start.18 = (f32[394]{0:T(512)}, f32[394]{0:T(512)S(1)}, u32[]{:S(2)}) copy-start(f32[394]{0:T(512)S(1)} %get-tuple-element.96) | copy-start | bytes 4732
  108.0 26.5 %all-to-all-start.2 = ((bf16[4,248,768]{2,1,0:T(8,128)(2,1)}), bf16[4,248,768]{2,1,0:T(8,128)(2,1)}, u32[]{:S(2)}, u32[]{:S(2)}) async-start(bf16[4,248,768]{2,1,0:T(8,128)(2,1)} %bitcast.132), calls=%async_computation.2 | async-start | bytes 3047424 | tf_op jit(solution)/shard_map/all_to_all | solution.py:117
  119.6 4.4 copy-start.56
  134.5 30.4 %all-to-all-start.1 = ((bf16[4,248,768]{2,1,0:T(8,128)(2,1)}), bf16[4,248,768]{2,1,0:T(8,128)(2,1)}, u32[]{:S(2)}, u32[]{:S(2)}) async-start(bf16[4,248,768]{2,1,0:T(8,128)(2,1)} %bitcast.133), calls=%async_computation.1 | async-start | bytes 3047424 | tf_op jit(solution)/shard_map/all_to_all | solution.py:97
  165.0 4.5 copy-start.40
  165.0 24.1 %all-to-all-start.3 = ((bf16[4,248,768]{2,1,0:T(8,128)(2,1)}), bf16[4,248,768]{2,1,0:T(8,128)(2,1)}, u32[]{:S(2)}, u32[]{:S(2)}) async-start(bf16[4,248,768]{2,1,0:T(8,128)(2,1)} %bitcast.130), calls=%async_computation.3 | async-start | bytes 3047424 | tf_op jit(solution)/shard_map/all_to_all | solution.py:137
  169.4 6.6 %copy-start.38 = (s32[2,394]{1,0:T(2,128)S(1)}, s32[2,394]{1,0:T(2,128)}, u32[]{:S(2)}) copy-start(s32[2,394]{1,0:T(2,128)} %copy-done.36) | copy-start | bytes 9460
  169.5 69.9 %reduce-scatter.10.cloned.1.call-start = ((), (), s32[]{:S(2)}) async-start(), calls=%async_computation.10 | async-start | bytes 1474560 | tf_op jit(solution)/shard_map/reduce_scatter | solution.py:222
  171.7 4.3 copy-start.51
  176.0 4.7 copy-start.22
  176.0 4.7 copy-start.19
  176.0 4.7 copy-start.26
  200.8 76.8 %reduce-scatter.8.cloned.1.call-start = ((), (), s32[]{:S(2)}) async-start(), calls=%async_computation.9 | async-start | bytes 4423680 | tf_op jit(solution)/shard_map/reduce_scatter | solution.py:219
  207.3 4.7 copy-start.15
  207.3 10.1 %slice-start = ((s8[4915200]{0:T(1024)(128)(4,1)}), s8[4194304]{0:T(1024)(128)(4,1)S(1)}, s32[]{:S(2)}) async-start(s8[4915200]{0:T(1024)(128)(4,1)} %bitcast.128), calls=%async_computation.15 | async-start | bytes 8388608
  212.0 5.3 slice-start.1
  235.8 96.7 %reduce-scatter.16.cloned.1.call-start = ((), (), s32[]{:S(2)}) async-start(), calls=%async_computation.13 | async-start | bytes 245760
  239.3 144.8 %all-reduce.10.cloned.1.call-start = ((), (), s32[]{:S(2)}) async-start(), calls=%async_computation.14 | async-start | bytes 2359296 | tf_op jit(solution)/shard_map/psum | solution.py:242
  277.6 204.8 %reduce-scatter.14.cloned.1.call-start = ((), (), s32[]{:S(2)}) async-start(), calls=%async_computation.12 | async-start | bytes 5308416 | tf_op jit(solution)/shard_map/reduce_scatter | solution.py:126
  289.4 291.8 %reduce-scatter.12.cloned.1.call-start = ((), (), s32[]{:S(2)}) async-start(), calls=%async_computation.11 | async-start | bytes 5308416 | tf_op jit(solution)/shard_map/reduce_scatter | solution.py:141
  298.6 6.2 %copy-start.41 = (f32[768]{0:T(1024)S(1)}, f32[768]{0:T(1024)}, u32[]{:S(2)}) copy-start(f32[768]{0:T(1024)} %param.16) | copy-start | bytes 9220
  298.6 6.2 %copy-start.44 = (f32[394]{0:T(512)S(1)}, f32[394]{0:T(512)}, u32[]{:S(2)}) copy-start(f32[394]{0:T(512)} %div.53) | copy-start | bytes 4732
  298.7 6.2 %copy-start.46 = (f32[394]{0:T(512)S(1)}, f32[394]{0:T(512)}, u32[]{:S(2)}) copy-start(f32[394]{0:T(512)} %rsqrt.21) | copy-start | bytes 4732
  304.9 5.9 copy-start.47
  326.9 6.4 %copy-start.53 = (bf16[192]{0:T(256)(128)(2,1)S(1)}, bf16[192]{0:T(256)(128)(2,1)}, u32[]{:S(2)}) copy-start(bf16[192]{0:T(256)(128)(2,1)} %dynamic-slice.3) | copy-start | bytes 1156
  (37 other events, 72.9 us)
Sparse Core Ops, SparseCore 0:
  200.9 26.7 reduce-scatter.9
  235.9 41.5 reduce-scatter.7
  280.6 19.7 reduce-scatter.15
  303.8 80.2 all-reduce.9
  387.6 94.7 reduce-scatter.13
  485.9 95.3 reduce-scatter.11
where the time goes:
time: 596 us; the launch traced here: 590 us
  waiting for transfers between devices  267 us (45%)
  matrix products  114 us (19%)
  local copies, waits for them, and re-layouts  100 us (17%)
  other arithmetic  46.6 us (8%)
  blocking collectives  28.9 us (5%)
  starting transfers between devices  18 us (3%)
  between operations  16.4 us (3%)
    reduce_scatter x1, waiting for transfers between devices, body(): lax.psum_scatter(jnp.einsum('rd,rf->df', columns, grad_pre, preferred_ele...  96.7 us
    reduce_scatter x1, waiting for transfers between devices, body(): lax.psum_scatter(jnp.einsum('rf,rd->fd', columns, grad_rows, preferred_el...  94 us
    unnamed x135, local copies, waits for them, and re-layouts  41.7 us
    reduce_scatter x1, waiting for transfers between devices, body(): lax.psum_scatter(shared[0].astype(jnp.bfloat16), 'ep', scatter_dimension=...  38.2 us
    psum x1, waiting for transfers between devices, body(): lax.psum(partial_sums[0].astype(jnp.bfloat16), 'dp').astype(jnp.float32)  23.1 us
    psum x1, blocking collectives, body(): lax.psum(partial_sums[3].astype(jnp.bfloat16), 'dp').astype(jnp.float32)  22.1 us
    dot_general x1, matrix products, body(): jnp.einsum('rd,fd->rf', grad_rows, w_out[0], preferred_element_type=jnp.f...  14.9 us
  transfers between devices with their start and end apart: 10, of which 6 were waited for; matrix products, arithmetic and copies ran while one was open for 27% of the time, Pallas kernels for 0%

commit v1 on v0

--- a/solution.py
+++ b/solution.py
@@ -1,29 +1,765 @@
+import contextlib
+import functools
+
 import jax
 import jax.numpy as jnp
 from jax import lax
+from jax.experimental import pallas as pl
+from jax.experimental.pallas import tpu as pltpu
 from jax.sharding import PartitionSpec as P
 
 HEADS = 12
 HEAD_DIM = 64
-
-
+MESH = pl.DeviceIdType.MESH
+BF = jnp.bfloat16
+F32 = jnp.float32
 eps = 1e-06
-
-
-def norm_forward(values):
-    centre = jnp.mean(values, axis=-1, keepdims=True)
-    shifted = values - centre
+NEG = -1e30
+LP = 256
+
+
+def dot(a, b):
+    return jnp.dot(a, b, preferred_element_type=F32)
+
+
+def dot_nt(a, b):
+    return lax.dot_general(a, b, (((1,), (1,)), ((), ())), preferred_element_type=F32)
+
+
+def dot_tn(a, b):
+    return lax.dot_general(a, b, (((0,), (0,)), ((), ())), preferred_element_type=F32)
+
+
+def lane(shape):
+    return lax.broadcasted_iota(jnp.int32, shape, len(shape) - 1)
+
+
+def sub(shape):
+    return lax.broadcasted_iota(jnp.int32, shape, len(shape) - 2)
+
+
+def norm_parts(v):
+    centre = jnp.mean(v, axis=-1, keepdims=True)
+    shifted = v - centre
     inverse = lax.rsqrt(jnp.mean(shifted * shifted, axis=-1, keepdims=True) + eps)
-    return (shifted * inverse, inverse)
-
-
-def norm_backward(grad_normed, normalized_input, inverse):
-    middle = jnp.mean(grad_normed, axis=-1, keepdims=True)
-    along = jnp.mean(grad_normed * normalized_input, axis=-1, keepdims=True)
-    return (grad_normed - middle - normalized_input * along) * inverse
-
-
-def body(
+    return shifted * inverse, inverse
+
+
+def norm_backward(y, n, inverse):
+    middle = jnp.mean(y, axis=-1, keepdims=True)
+    along = jnp.mean(y * n, axis=-1, keepdims=True)
+    return (y - middle - n * along) * inverse
+
+
+def sc(name):
+    return contextlib.nullcontext()
+
+
+COPIES = {}
+for _name, _count in (
+    ("uP", 2), ("uO", 2), ("uF", 2), ("sP", 1), ("sO", 1), ("sF", 1), ("gP", 2), ("gO", 2), ("gF", 2),
+    ("ox", 4), ("oz", 3), ("ix", 4), ("iz", 12),
+    ("dP", 2), ("dD", 2), ("dO", 2), ("eP", 1), ("eD", 1), ("eO", 1), ("yP", 2), ("yD", 2), ("yO", 2),
+    ("C", 8), ("Y", 4), ("X", 4), ("Z", 12), ("AZ", 12), ("AX", 4), ("mC", 2), ("mY", 1), ("mX", 1), ("mZ", 3),
+):
+    COPIES[_name] = sum(n for _, n in COPIES.values()), _count
+N_COPIES = sum(n for _, n in COPIES.values())
+
+
+def layer_kernel(
+    experts, seq, live, routes, gains, wrt, xb, gl, w_in, w_out, wqkv, wo,
+    bo_o, DH, sm_o, wo_o, wi_o, sg_o, qa_h, c_h,
+    U, G, SL, WR, WI, WO, M, D, X, GE, DT,
+    GOs, GOk, GOx, GOz, GIs, GIk, GIx, GIz,
+    H, LS, GD, RP, RD, RO, EP, ED, EO, ES, YP, YD, YO, SM, SMx,
+    ssem, rsem, lsem, free,
+):
+    f, width = WO.shape
+    sp, rows, half_rows = 208, 416, 512
+    shard, block = width // 4, width // 16
+    dp, ep = lax.axis_index("dp"), lax.axis_index("ep")
+    z, x = dp // 2, dp % 2
+    y, core = ep // 2, ep % 2
+    to_p = {"ep": y * 2 + 1 - core}
+    to_o = {"ep": (1 - y) * 2 + core}
+    to_x = {"dp": z * 2 + 1 - x}
+    zs = [lax.rem(z + k, 4) for k in range(4)]
+    to_z = [{"dp": zs[k] * 2 + x} for k in range(4)]
+    friends = (to_p, to_o, to_x, to_z[1], to_z[2], to_z[3])
+    g1, b1, g2, b2 = (gains[n:n + 1, :] for n in range(4))
+
+    def rc(name, i, src, dst, dev):
+        at = COPIES[name][0] + i
+        return pltpu.make_async_remote_copy(
+            src_ref=src, dst_ref=dst, send_sem=ssem.at[at], recv_sem=rsem.at[at], device_id=dev, device_id_type=MESH)
+
+    def lc(i, src, dst):
+        return pltpu.make_async_copy(src, dst, lsem.at[i])
+
+    top = pl.ds(0, sp)
+    barrier = pltpu.get_barrier_semaphore()
+    for dev in friends:
+        pl.semaphore_signal(barrier, inc=1, device_id=dev, device_id_type=MESH)
+
+    def attention_weights(first):
+        cps = [lc(first + n, wqkv.at[:, pl.ds(n * width, width)], WO.at[pl.ds(n * width, width)]) for n in range(3)]
+        return cps + [lc(first + 3, wo, WO.at[pl.ds(3 * width, width)])]
+
+    load_x = [lc(i, xb.at[i], GE.at[pl.ds(i * sp, sp)]) for i in range(2)]
+    load_w = attention_weights(2)
+    load_g = [lc(6 + i, gl.at[i], G.at[0, i, top]) for i in range(2)]
+    load_in = lc(8, w_in.at[0], WI)
+    for cp in load_x + load_w + load_g + [load_in]:
+        cp.start()
+
+    shape = SL.shape[2:]
+    before = (sub((LP, LP)) < lane((LP, LP))).astype(BF)
+    base = jnp.zeros((shape[0], 1), F32)
+    for i in range(2):
+        r = jnp.concatenate([routes[i], jnp.full((2, LP - seq), -1, jnp.int32)], axis=1)
+        member = (r[0:1, :] == sub(shape)) | (r[1:2, :] == sub(shape))
+        member = member & (live[0] > i)
+        m = member.astype(F32)
+        place = dot(m.astype(BF), before) + base
+        SL[0, i] = jnp.where(member, place, -1.0)
+        base = base + jnp.sum(m, axis=1, keepdims=True)
+    WR[...] = jnp.zeros(WR.shape, BF)
+    WR[0:experts, :] = wrt[...]
+    for s in range(4):
+        for i in range(2):
+            U[s, i, sp:, :] = jnp.zeros((LP - sp, width), BF)
+            G[s, i, sp:, :] = jnp.zeros((LP - sp, width), BF)
+
+    uP = [rc("uP", i, U.at[0, i, top], U.at[1, i, top], to_p) for i in range(2)]
+    uO = [rc("uO", i, U.at[0, i, top], U.at[2, i, top], to_o) for i in range(2)]
+    uF = [rc("uF", i, U.at[2, i, top], U.at[3, i, top], to_p) for i in range(2)]
+    gP = [rc("gP", i, G.at[0, i, top], G.at[1, i, top], to_p) for i in range(2)]
+    gO = [rc("gO", i, G.at[0, i, top], G.at[2, i, top], to_o) for i in range(2)]
+    gF = [rc("gF", i, G.at[2, i, top], G.at[3, i, top], to_p) for i in range(2)]
+    sP = rc("sP", 0, SL.at[0], SL.at[1], to_p)
+    sO = rc("sO", 0, SL.at[0], SL.at[2], to_o)
+    sF = rc("sF", 0, SL.at[2], SL.at[3], to_p)
+
+    low = lane((sp, 128)) < HEAD_DIM
+    keys = lane((sp, sp)) < seq
+    scaling = HEAD_DIM ** -0.5
+    with sc("ln1"):
+        for i in range(2):
+            load_x[i].wait()
+            r0 = slice(i * sp, (i + 1) * sp)
+            n1, _ = norm_parts(GE[r0, :].astype(F32))
+            D[r0, 3 * width:] = (n1 * g1 + b1).astype(BF)
+    with sc("qkv"):
+        for n in range(3):
+            load_w[n].wait()
+            D[0:rows, n * width:(n + 1) * width] = dot(
+                D[0:rows, 3 * width:], WO[n * width:(n + 1) * width, :]).astype(BF)
+    with sc("barrier"):
+        pl.semaphore_wait(barrier, 6)
+    sO.start()
+    sP.start()
+    load_g[0].wait()
+    gO[0].start()
+    gP[0].start()
+    LS[...] = jnp.zeros(LS.shape, F32)
+
+    def attend(i, per):
+        r0 = slice(i * sp, (i + 1) * sp)
+
+        def pair(step, carry):
+            lse = LS[i]
+            for inner in range(per):
+                h = step * per + inner
+
+                def cols(n):
+                    return pl.ds(pl.multiple_of(h * 128 + n * width, 128), 128)
+
+                q, k, v = D[r0, cols(0)], D[r0, cols(1)], D[r0, cols(2)]
+                outs = []
+                for side in range(2):
+                    mine = low if side == 0 else ~low
+                    s = dot_nt(jnp.where(mine, q, jnp.zeros_like(q)), k) * scaling
+                    s = jnp.where(keys, s, NEG)
+                    peak = jnp.max(s, axis=-1, keepdims=True)
+                    e = jnp.exp(s - peak)
+                    total = jnp.sum(e, axis=-1, keepdims=True)
+                    lse = jnp.where(lane((sp, 128)) == 2 * h + side, peak + jnp.log(total), lse)
+                    outs.append(dot((e / total).astype(BF), v))
+                D[rows + i * sp:rows + (i + 1) * sp, cols(0)] = jnp.where(low, outs[0], outs[1]).astype(BF)
+            LS[i] = lse
+            return carry
+
+        lax.fori_loop(0, width // 128 // per, pair, 0)
+
+    for i in range(2):
+        with sc("attend"):
+            attend(i, 2)
+        with sc("proj_ln2"):
+            if i == 0:
+                load_w[3].wait()
+            r1 = slice(rows + i * sp, rows + (i + 1) * sp)
+            h1 = GE[i * sp:(i + 1) * sp, :].astype(F32) + dot(D[r1, 0:width], WO[3 * width:, :])
+            H[i] = h1
+            n2, _ = norm_parts(h1)
+            U[0, i, :sp, :] = (n2 * g2 + b2).astype(BF)
+        uO[i].start()
+        uP[i].start()
+    load_g[1].wait()
+    gO[1].start()
+    gP[1].start()
+    keep = [lc(0, D.at[pl.ds(0, rows)], qa_h), lc(1, D.at[pl.ds(rows, rows), pl.ds(0, width)], c_h)]
+    load_out = lc(2, w_out.at[0], WO)
+    for cp in keep + [load_out]:
+        cp.start()
+
+    def onehot(s):
+        want = sub((LP, LP)).astype(F32)
+        parts = [(want == SL[s, i, pl.ds(ep, 1), :]).astype(BF) for i in range(2)]
+        return jnp.concatenate(parts, axis=1)
+
+    def gather(s):
+        X[s * LP:(s + 1) * LP, :] = dot(onehot(s), U[s].reshape(2 * LP, width)).astype(BF)
+
+    tile = 512
+    tiles = f // tile
+    c0 = 0.7978845608028654
+    c1 = c0 * 0.044715
+
+    def expert_in(first):
+        rs = slice(first, first + half_rows)
+
+        def step(n, carry):
+            cols = pl.ds(pl.multiple_of(n * tile, tile), tile)
+            v = dot(X[rs, :], WI[:, cols])
+            w = v * v
+            t = jnp.tanh(v * (c0 + c1 * w))
+            h = 0.5 + 0.5 * t
+            M[rs, cols] = (v * h).astype(BF)
+            D[rs, cols] = (h + h * (1.0 - t) * (v * (c0 + 3.0 * c1 * w))).astype(BF)
+            return carry
+
+        lax.fori_loop(0, tiles, step, 0)
+        r = dot_nt(X[rs, :], WR[...])
+        r = jnp.where(lane(r.shape) < experts, r, NEG)
+        r = jnp.exp(r - jnp.max(r, axis=-1, keepdims=True))
+        r = r / jnp.sum(r, axis=-1, keepdims=True)
+        GD[rs, 0:1] = jnp.sum(jnp.where(lane(r.shape) == ep, r, 0.0), axis=-1, keepdims=True)
+
+    def gather_grads(s):
+        rs = slice(s * LP, (s + 1) * LP)
+        got = dot(onehot(s), G[s].reshape(2 * LP, width))
+        GE[rs, :] = got.astype(BF)
+        DT[:, rs] = jnp.transpose(GD[rs, 0:1] * got).astype(BF)
+
+    with sc("wait_uP"):
+        gather(0)
+        sP.wait_recv()
+        for i in range(2):
+            uP[i].wait_recv()
+        gather(1)
+        load_in.wait()
+        for cp in keep:
+            cp.wait()
+    with sc("expert_in_0"):
+        expert_in(0)
+    with sc("wait_g0"):
+        sO.wait_recv()
+        sF.start()
+        gO[0].wait_recv()
+        gF[0].start()
+    with sc("wait_uO"):
+        for i in range(2):
+            uO[i].wait_recv()
+            uF[i].start()
+        gather(2)
+    with sc("wait_uF"):
+        sF.wait_recv()
+        for i in range(2):
+            uF[i].wait_recv()
+        gather(3)
+    with sc("expert_in_1"):
+        expert_in(half_rows)
+    with sc("wait_gP"):
+        for i in range(2):
+            gP[i].wait_recv()
+        gather_grads(0)
+        gather_grads(1)
+    with sc("wait_gO"):
+        gO[1].wait_recv()
+        gF[1].start()
+        gather_grads(2)
+    with sc("wait_gF"):
+        for i in range(2):
+            gF[i].wait_recv()
+        gather_grads(3)
+
+    def ox(t):
+        return rc("ox", t, GOs.at[t], GOx.at[t], to_x)
+
+    def oz(k):
+        return rc("oz", k - 1, GOk.at[k - 1], GOz.at[k - 1], to_z[k])
+
+    def ix(j):
+        return rc("ix", j, GIs.at[j], GIx.at[j], to_x)
+
+    def iz(j, k):
+        return rc("iz", j * 3 + k - 1, GIk.at[j, zs[k]], GIz.at[k - 1, j], to_z[k])
+
+    def w_out_tile(t, carry):
+        zp = lax.rem(z + 1 + t, 4)
+        r = dot(DT[...], M[:, pl.ds(pl.multiple_of(zp * width, width), width)])
+        lo, hi = r[:, :width // 2], r[:, width // 2:]
+        GOs[t] = jnp.where(x == 0, hi, lo).astype(BF)
+        GOk[t] = jnp.where(x == 0, lo, hi).astype(BF)
+        ox(t).start()
+        return carry
+
+    with sc("w_out_tiles"):
+        lax.fori_loop(0, 4, w_out_tile, 0)
+
+    def take_o(t):
+        with sc("take_o%d" % t):
+            ox(t).wait_recv()
+            GOk[t] = (GOk[t].astype(F32) + GOx[t].astype(F32)).astype(BF)
+            if t < 3:
+                oz(t + 1).start()
+
+    def take_i(j):
+        with sc("take_i%d" % j):
+            ix(j).wait_recv()
+            GIk[j] = (GIk[j].astype(F32) + GIx[j].astype(F32)).astype(BF)
+            for k in range(1, 4):
+                iz(j, k).start()
+
+    load_out.wait()
+    GD[:, 1:2] = jnp.zeros((GD.shape[0], 1), F32)
+
+    def expert_back(n, carry):
+        cols = pl.ds(pl.multiple_of(n * tile, tile), tile)
+        for first in (0, half_rows):
+            rs = slice(first, first + half_rows)
+            back = dot_nt(GE[rs, :], WO[cols, :])
+            GD[rs, 1:2] += jnp.sum(back * M[rs, cols].astype(F32), axis=-1, keepdims=True)
+            D[rs, cols] = (D[rs, cols].astype(F32) * (GD[rs, 0:1] * back)).astype(BF)
+        return carry
+
+    with sc("expert_back"):
+        lax.fori_loop(0, tiles, expert_back, 0)
+    take_o(0)
+
+    dP = [rc("dP", i, U.at[1, i, top], RP.at[i], to_p) for i in range(2)]
+    dD = [rc("dD", i, U.at[3, i, top], RD.at[i], to_p) for i in range(2)]
+    dO = [rc("dO", i, U.at[2, i, top], RO.at[i], to_o) for i in range(2)]
+    eP = rc("eP", 0, ES.at[1], EP, to_p)
+    eD = rc("eD", 0, ES.at[3], ED, to_p)
+    eO = rc("eO", 0, ES.at[2], EO, to_o)
+    yP = [rc("yP", i, G.at[1, i, top], YP.at[i], to_p) for i in range(2)]
+    yD = [rc("yD", i, G.at[3, i, top], YD.at[i], to_p) for i in range(2)]
+    yO = [rc("yO", i, G.at[2, i, top], YO.at[i], to_o) for i in range(2)]
+
+    for cp in uP + uO + uF:
+        cp.wait_send()
+
+    def scatter(s, values):
+        return dot_tn(onehot(s), values)
+
+    for s in (3, 2, 1, 0):
+        with sc("du%d" % s):
+            rs = slice(s * LP, (s + 1) * LP)
+            out = scatter(s, dot_nt(D[rs, :], WI[...]).astype(BF))
+            if s == 0:
+                for i in range(2):
+                    DH[i] = out[i * LP:i * LP + sp]
+            else:
+                U[s] = out.astype(BF).reshape(2, LP, width)
+            dg = GD[rs, 1:2]
+            hi = dg.astype(BF)
+            rest = (dg - hi.astype(F32)).astype(BF)
+            at = lane((LP, 128))
+            zero = jnp.zeros((LP, 128), BF)
+            two = jnp.where(at == ep, hi, zero) + jnp.where(at == ep + 64, rest, zero)
+            ES[s] = scatter(s, two).astype(BF).reshape(2, LP, 128)
+            if s == 3:
+                for cp in dD + [eD]:
+                    cp.start()
+            if s == 1:
+                for cp in dP + [eP]:
+                    cp.start()
+    with sc("combine_du"):
+        for i in range(2):
+            dD[i].wait_recv()
+            U[2, i, :sp, :] = (U[2, i, :sp, :].astype(F32) + RD[i].astype(F32)).astype(BF)
+            dO[i].start()
+        eD.wait_recv()
+        ES[2] = ES[2] + ED[...]
+        eO.start()
+    take_o(1)
+
+    def w_in_tile(j, carry):
+        r = dot_tn(X[...], D[:, pl.ds(pl.multiple_of(j * width, width), width)]).reshape(4, 2, width // 8, width)
+        first, second = r[:, 0], r[:, 1]
+        GIs[j] = jnp.where(x == 0, second, first).astype(BF)
+        GIk[j] = jnp.where(x == 0, first, second).astype(BF)
+        ix(j).start()
+        return carry
+
+    with sc("w_in_tiles"):
+        lax.fori_loop(0, 4, w_in_tile, 0)
+    for dev in friends:
+        pl.semaphore_signal(free, inc=1, device_id=dev, device_id_type=MESH)
+
+    for cp in gP + gO + gF:
+        cp.wait_send()
+    for s in (3, 2, 1, 0):
+        with sc("o%d" % s):
+            rs = slice(s * LP, (s + 1) * LP)
+            o = dot(M[rs, :], WO[...]).astype(BF).astype(F32)
+            out = scatter(s, (GD[rs, 0:1] * o).astype(BF)).astype(BF)
+            if s == 0:
+                X[0:half_rows, :] = out
+            else:
+                G[s] = out.reshape(2, LP, width)
+            if s == 3:
+                for cp in yD:
+                    cp.start()
+            if s == 1:
+                for cp in yP:
+                    cp.start()
+    late = attention_weights(3) + [
+        lc(7, qa_h, M.at[pl.ds(0, rows)]), lc(8, c_h, M.at[pl.ds(rows, rows), pl.ds(0, width)])
+    ] + [lc(9 + i, xb.at[i], GE.at[pl.ds(rows + i * sp, sp)]) for i in range(2)]
+    for cp in late:
+        cp.start()
+    with sc("combine_y"):
+        for i in range(2):
+            yD[i].wait_recv()
+            G[2, i, :sp, :] = (G[2, i, :sp, :].astype(F32) + YD[i].astype(F32)).astype(BF)
+            yO[i].start()
+    take_o(2)
+
+    with sc("wait_du"):
+        for i in range(2):
+            dP[i].wait_recv()
+            dO[i].wait_recv()
+        eP.wait_recv()
+        eO.wait_recv()
+    with sc("ln2_back"):
+        router = jnp.zeros((width, 128), F32)
+        gain2 = jnp.zeros((1, width), F32)
+        bias2 = jnp.zeros((1, width), F32)
+        for i in range(2):
+            du = DH[i] + RP[i].astype(F32) + RO[i].astype(F32)
+            back = ES[0, i, :sp, :].astype(F32) + EP[i, :sp, :].astype(F32) + EO[i, :sp, :].astype(F32)
+            back = back + pltpu.roll(back, 64, axis=1)
+            own = U[0, i, :sp, :]
+            r = dot_nt(own, WR[...])
+            r = jnp.where(lane(r.shape) < experts, r, NEG)
+            r = jnp.exp(r - jnp.max(r, axis=-1, keepdims=True))
+            r = r / jnp.sum(r, axis=-1, keepdims=True)
+            dl = (r * (back - jnp.sum(r * back, axis=-1, keepdims=True))).astype(BF)
+            router = router + dot_tn(own, dl)
+            du = du + dot(dl, WR[...])
+            n2, inv2 = norm_parts(H[i])
+            gain2 = gain2 + jnp.sum(du * n2, axis=0, keepdims=True)
+            bias2 = bias2 + jnp.sum(du, axis=0, keepdims=True)
+            dh = G[0, i, :sp, :].astype(F32) + norm_backward(du * g2, n2, inv2)
+            DH[i] = dh
+            GE[i * sp:(i + 1) * sp, :] = dh.astype(BF)
+        SM[...] = router.astype(BF)
+    for cp in late:
+        cp.wait()
+
+    def part(e, b):
+        return pl.ds(pl.multiple_of(e * shard, shard), shard), pl.ds(b * width, width)
+
+    def mine(b, h):
+        return pl.ds(pl.multiple_of(b * width + h * (width // 2), 128), width // 2)
+
+    def rest(r0, n, b, second):
+        return D.at[r0:r0 + n, pl.ds(b * width + second * (width // 2), width // 2)]
+
+    def cp_c(b, i):
+        return rc("C", b * 2 + i, WI.at[part(i * 2 + 1 - core, b)], D.at[pl.ds(i * shard, shard), pl.ds(b * width, width)], to_p)
+
+    def cp_y(b):
+        return rc("Y", b, WI.at[part((1 - y) * 2 + core, b)], D.at[pl.ds(2 * shard, shard), pl.ds(b * width, width)], to_o)
+
+    def own_rows(k=0, n=shard):
+        return pl.ds(pl.multiple_of(ep * shard + k * block, block), n)
+
+    def cp_x(b):
+        return rc("X", b, WI.at[own_rows(), mine(b, 1 - x)], rest(3 * shard, shard, b, 0), to_x)
+
+    def cp_z(b, k):
+        return rc("Z", b * 3 + k - 1, WI.at[own_rows(zs[k], block), mine(b, x)],
+                  rest(4 * shard + (k - 1) * block, block, b, 0), to_z[k])
+
+    def result(k, b):
+        return D.at[pl.ds(pl.multiple_of(4 * shard + k * block, block), block),
+                    pl.ds(b * width + width // 2, width // 2)]
+
+    def cp_az(b, k):
+        return rc("AZ", b * 3 + k - 1, result(z, b), result(z, b), to_z[k])
+
+    def cp_ax(b):
+        return rc("AX", b, rest(4 * shard, shard, b, 1), rest(3 * shard, shard, b, 1), to_x)
+
+    def stage_c(b):
+        for i in range(2):
+            cp_c(b, i).start()
+
+    def stage_y(b):
+        with sc("stage_y%d" % b):
+            for i in range(2):
+                cp_c(b, i).wait_recv()
+            for i in range(2):
+                at = part(i * 2 + core, b)
+                WI[at] = (WI[at].astype(F32) + D[i * shard:(i + 1) * shard, b * width:(b + 1) * width].astype(F32)).astype(BF)
+            cp_y(b).start()
+
+    def stage_x(b):
+        with sc("stage_x%d" % b):
+            cp_y(b).wait_recv()
+            at = part(ep, b)
+            WI[at] = (WI[at].astype(F32) + D[2 * shard:3 * shard, b * width:(b + 1) * width].astype(F32)).astype(BF)
+            cp_x(b).start()
+
+    def stage_z(b):
+        with sc("stage_z%d" % b):
+            cp_x(b).wait_recv()
+            at = own_rows(), mine(b, x)
+            WI[at] = (WI[at].astype(F32) + rest(3 * shard, shard, b, 0)[...].astype(F32)).astype(BF)
+            for k in range(1, 4):
+                cp_z(b, k).start()
+
+    def stage_az(b):
+        with sc("stage_az%d" % b):
+            for k in range(1, 4):
+                cp_z(b, k).wait_recv()
+            total = WI[own_rows(z, block), mine(b, x)].astype(F32)
+            for k in range(3):
+                total = total + rest(4 * shard + k * block, block, b, 0)[...].astype(F32)
+            result(z, b)[...] = total.astype(BF)
+            for k in range(1, 4):
+                cp_az(b, k).start()
+
+    def stage_ax(b):
+        with sc("stage_ax%d" % b):
+            for k in range(1, 4):
+                rc("AZ", b * 3 + k - 1, result(zs[4 - k], b), result(zs[4 - k], b), to_z[k]).wait_recv()
+            cp_ax(b).start()
+
+    with sc("attn_out_grads"):
+        X[half_rows:half_rows + rows, :] = dot_nt(GE[0:rows, :], WO[3 * width:, :]).astype(BF)
+        WI[:, 3 * width:] = dot_tn(M[rows:2 * rows, 0:width], GE[0:rows, :]).astype(BF)
+    with sc("wait_free"):
+        pl.semaphore_wait(free, 6)
+    stage_c(3)
+    take_o(3)
+
+    def pair_back(h, carry):
+        def cols(n):
+            return pl.ds(pl.multiple_of(h * 128 + n * width, 128), 128)
+
+        for i in range(2):
+            r0 = slice(i * sp, (i + 1) * sp)
+            q, k, v = M[r0, cols(0)], M[r0, cols(1)], M[r0, cols(2)]
+            dc = X[half_rows + i * sp:half_rows + (i + 1) * sp, cols(0)]
+            parts = []
+            for side in range(2):
+                here = low if side == 0 else ~low
+                zero = jnp.zeros_like(q)
+                lse = jnp.sum(jnp.where(lane((sp, 128)) == 2 * h + side, LS[i], 0.0), axis=-1, keepdims=True)
+                s = dot_nt(jnp.where(here, q, zero), k) * scaling
+                p = jnp.exp(jnp.where(keys, s, NEG) - lse)
+                dv = dot_tn(p.astype(BF), dc)
+                dp_ = dot_nt(jnp.where(here, dc, zero), v)
+                ds = (p * (dp_ - jnp.sum(p * dp_, axis=-1, keepdims=True))).astype(BF)
+                parts.append((dot(ds, k) * scaling, dot_tn(ds, q) * scaling, dv))
+            r1 = slice(rows + i * sp, rows + (i + 1) * sp)
+            for n in range(3):
+                M[r1, cols(n + 1)] = jnp.where(low, parts[0][n], parts[1][n]).astype(BF)
+        return carry
+
+    with sc("attention_back_a"):
+        lax.fori_loop(0, width // 256, pair_back, 0)
+    stage_y(3)
+    take_i(0)
+    with sc("attention_back_b"):
+        lax.fori_loop(width // 256, width // 128, pair_back, 0)
+    for n in range(3):
+        with sc("qkv_grads"):
+            grads = M[rows:2 * rows, (n + 1) * width:(n + 2) * width]
+            WI[:, n * width:(n + 1) * width] = dot_tn(M[0:rows, 3 * width:], grads).astype(BF)
+        stage_c(n)
+    stage_x(3)
+    with sc("ln1_back"):
+        gain1 = jnp.zeros((1, width), F32)
+        bias1 = jnp.zeros((1, width), F32)
+        for i in range(2):
+            r1 = slice(rows + i * sp, rows + (i + 1) * sp)
+            grad = dot_nt(M[r1, width:2 * width], WO[0:width, :])
+            for n in range(1, 3):
+                grad = grad + dot_nt(M[r1, (n + 1) * width:(n + 2) * width], WO[n * width:(n + 1) * width, :])
+            n1, inv1 = norm_parts(GE[r1, :].astype(F32))
+            gain1 = gain1 + jnp.sum(grad * n1, axis=0, keepdims=True)
+            bias1 = bias1 + jnp.sum(grad, axis=0, keepdims=True)
+            DH[i] = DH[i] + norm_backward(grad * g1, n1, inv1)
+        vectors = jnp.concatenate([jnp.zeros((4, width), F32), gain1, bias1, gain2, bias2], axis=0)
+        vectors = jnp.concatenate([vectors, jnp.zeros((120, width), F32)], axis=0)
+        SM[...] = (SM[...].astype(F32) + jnp.transpose(vectors)).astype(BF)
+
+    def small(e):
+        return pl.ds(pl.multiple_of(e * shard, shard), shard)
+
+    mC = [rc("mC", i, SM.at[small(i * 2 + 1 - core)], SMx.at[i], to_p) for i in range(2)]
+    mY = rc("mY", 0, SM.at[small((1 - y) * 2 + core)], SMx.at[2], to_o)
+    mX = rc("mX", 0, SM.at[small(ep)], SMx.at[3], to_x)
+    mZ = [rc("mZ", k - 1, SMx.at[3], SMx.at[3 + k], to_z[k]) for k in range(1, 4)]
+    for cp in mC:
+        cp.start()
+    for b in range(3):
+        stage_y(b)
+    with sc("small_y"):
+        for i in range(2):
+            mC[i].wait_recv()
+            at = small(i * 2 + core)
+            SM[at, :] = (SM[at, :].astype(F32) + SMx[i].astype(F32)).astype(BF)
+        mY.start()
+    with sc("block_out"):
+        for i in range(2):
+            yP[i].wait_recv()
+            yO[i].wait_recv()
+            on = (live[0] > i).astype(F32)
+            mix = X[i * LP:i * LP + sp, :].astype(F32) + YP[i].astype(F32) + YO[i].astype(F32)
+            bo_o[i] = ((H[i] + mix) * on).astype(BF)
+    take_i(1)
+    stage_x(0)
+    take_i(2)
+    stage_x(1)
+    stage_z(3)
+    stage_x(2)
+    with sc("small_x"):
+        mY.wait_recv()
+        at = small(ep)
+        SM[at, :] = (SM[at, :].astype(F32) + SMx[2].astype(F32)).astype(BF)
+        mX.start()
+    take_i(3)
+    with sc("small_z"):
+        mX.wait_recv()
+        SMx[3] = (SM[small(ep), :].astype(F32) + SMx[3].astype(F32)).astype(BF)
+        for cp in mZ:
+            cp.start()
+    stage_az(3)
+    for b in range(3):
+        stage_z(b)
+    stage_ax(3)
+    for b in range(3):
+        stage_az(b)
+    with sc("o_sum"):
+        for k in range(1, 4):
+            oz(k).wait_recv()
+        total = GOk[3].astype(F32)
+        for k in range(3):
+            total = total + GOz[k].astype(F32)
+        GOk[3] = total.astype(BF)
+        outs = [lc(0, GOk.at[3], wo_o)]
+        outs[0].start()
+    for j in range(4):
+        with sc("i_sum"):
+            for k in range(1, 4):
+                iz(j, k).wait_recv()
+            total = GIk[j, z].astype(F32)
+            for k in range(3):
+                total = total + GIz[k, j].astype(F32)
+            GIx[j, 0] = total.astype(BF)
+            outs.append(lc(1 + j, GIx.at[j, 0], wi_o.at[:, pl.ds(j * width, width)]))
+            outs[-1].start()
+    with sc("small_sum"):
+        for cp in mZ:
+            cp.wait_recv()
+        total = SMx[3].astype(F32) + SMx[4].astype(F32) + SMx[5].astype(F32) + SMx[6].astype(F32)
+        sm_o[...] = jnp.transpose(total)[0:8, :]
+    for b in range(3):
+        stage_ax(b)
+    for b in (3, 0, 1, 2):
+        outs.append(lc(5 + b, rest(4 * shard, shard, b, 1), sg_o.at[:, mine(b, x)]))
+        outs[-1].start()
+    with sc("wait_ax"):
+        for b in (3, 0, 1, 2):
+            cp_ax(b).wait_recv()
+            outs.append(lc(9 + b, rest(3 * shard, shard, b, 1), sg_o.at[:, mine(b, 1 - x)]))
+            outs[-1].start()
+    with sc("drain"):
+        for cp in dP + dD + dO + yP + yD + yO + [sP, sO, sF, eP, eD, eO, mY, mX] + mC + mZ:
+            cp.wait_send()
+        for t in range(4):
+            ox(t).wait_send()
+            ix(t).wait_send()
+            cp_y(t).wait_send()
+            cp_x(t).wait_send()
+            cp_ax(t).wait_send()
+            for i in range(2):
+                cp_c(t, i).wait_send()
+            for k in range(1, 4):
+                iz(t, k).wait_send()
+                cp_z(t, k).wait_send()
+                cp_az(t, k).wait_send()
+        for k in range(1, 4):
+            oz(k).wait_send()
+        for cp in outs:
+            cp.wait()
+
+
+def fast_body(n_ep, tokens, live, routes, g1, b1, wqkv, wo, g2, b2, wr, w_in, w_out, cot):
+    slots, seq, width = tokens.shape
+    sp = (seq + 15) // 16 * 16
+    f = w_in.shape[2]
+    cap = n_ep * LP
+    pads = ((0, 0), (0, sp - seq), (0, 0))
+    on = (jnp.arange(slots, dtype=jnp.int32) < live[0])[:, None, None]
+    gl = jnp.pad(jnp.where(on, cot, jnp.zeros_like(cot)), pads)
+    xb = jnp.pad(tokens, pads)
+    gains = jnp.stack([g1, b1, g2, b2])
+    sds = jax.ShapeDtypeStruct
+    vm = pl.BlockSpec(memory_space=pltpu.VMEM)
+    anys = pl.BlockSpec(memory_space=pl.ANY)
+    b = lambda *shape: pltpu.VMEM(shape, BF)
+    g = lambda *shape: pltpu.VMEM(shape, F32)
+    shard = width // n_ep
+    bo, gt, sm, wo_t, wi, sg, _, _ = pl.pallas_call(
+        functools.partial(layer_kernel, n_ep, seq),
+        name="layer",
+        out_shape=(
+            sds((slots, sp, width), BF), sds((slots, sp, width), F32), sds((8, shard), F32),
+            sds((width, f // 8), BF), sds((width // 8, f), BF), sds((shard, 4 * width), BF),
+            sds((2 * sp, 4 * width), BF), sds((2 * sp, width), BF),
+        ),
+        in_specs=[pl.BlockSpec(memory_space=pltpu.SMEM)] + [vm] * 3 + [anys] * 6,
+        out_specs=[vm] * 3 + [anys] * 5,
+        scratch_shapes=[
+            b(4, 2, LP, width), b(4, 2, LP, width), g(4, 2, 8, LP), b(128, width), b(width, f), b(f, width),
+            b(cap, f), b(cap, f), b(cap, width), b(cap, width), b(width, cap),
+            b(4, width, f // 8), b(4, width, f // 8), b(4, width, f // 8), b(3, width, f // 8),
+            b(4, 4, width // 8, width), b(4, 4, width // 8, width), b(4, 4, width // 8, width),
+            b(3, 4, width // 8, width),
+            g(slots, sp, width), g(slots, sp, 128), g(cap, 2),
+            b(2, sp, width), b(2, sp, width), b(2, sp, width),
+            b(2, LP, 128), b(2, LP, 128), b(2, LP, 128), b(4, 2, LP, 128),
+            b(2, sp, width), b(2, sp, width), b(2, sp, width), b(width, 128), b(7, shard, 128),
+            pltpu.SemaphoreType.DMA((N_COPIES,)), pltpu.SemaphoreType.DMA((N_COPIES,)),
+            pltpu.SemaphoreType.DMA((14,)), pltpu.SemaphoreType.REGULAR,
+        ],
+        compiler_params=pltpu.CompilerParams(
+            collective_id=0, has_side_effects=True, vmem_limit_bytes=67043328),
+    )(live, jnp.transpose(routes, (0, 2, 1)), gains, jnp.transpose(wr), xb, gl, w_in, w_out, wqkv, wo)
+    return (
+        bo[:, :seq], gt[:, :seq], sm[4], sm[5], sg[:, :3 * width].astype(F32), sg[:, 3 * width:].astype(F32),
+        sm[6], sm[7], jnp.transpose(sm[:n_ep]), wi.astype(F32)[None], jnp.transpose(wo_t).astype(F32)[None],
+    )
+
+
+def general_body(
     tokens,
     live_images,
     routes,
@@ -45,7 +781,7 @@
     capacity = ((2 * row_count + expert_count - 1) // expert_count * 5 // 4 + 7) // 8 * 8
     scaling = HEAD_DIM ** (-0.5)
     inputs = tokens.astype(jnp.float32).reshape(row_count, model_width)
-    normed1, inverse1 = norm_forward(inputs)
+    normed1, inverse1 = norm_parts(inputs)
     attn_in = (normed1 * ln1_gain + ln1_bias).astype(jnp.bfloat16)
     qkv_rows = jnp.dot(attn_in, query_key_value_weight, preferred_element_type=jnp.float32).astype(
         jnp.bfloat16
@@ -70,7 +806,7 @@
     hidden1 = inputs + jnp.dot(
         attended_context, attention_output_weight, preferred_element_type=jnp.float32
     )
-    normed2, inverse2 = norm_forward(hidden1)
+    normed2, inverse2 = norm_parts(hidden1)
     moe_in = (normed2 * ln2_gain + ln2_bias).astype(jnp.bfloat16)
     router = jax.nn.softmax(jnp.dot(moe_in, w_router, preferred_element_type=jnp.float32), axis=-1)
     chosen = routes.reshape(row_count, 2)
@@ -291,4 +1027,6 @@
         P("ep", "dp", None),
         P("ep", "dp", None),
     )
+    n_dp, n_ep = mesh.shape["dp"], mesh.shape["ep"]
+    body = functools.partial(fast_body, n_ep) if (n_dp, n_ep) == (8, 4) else general_body
     return jax.shard_map(body, mesh=mesh, in_specs=in_specs, out_specs=out_specs, check_vma=False)

time: 596 us -> 225 us (0.38)
  waiting for transfers between devices: 267 us -> 0 us
  Pallas kernels: 0 us -> 203 us
  matrix products: 114 us -> 0 us
  local copies, waits for them, and re-layouts: 100 us -> 11.5 us
  other arithmetic: 46.6 us -> 5.23 us
  blocking collectives: 28.9 us -> 0 us
  starting transfers between devices: 18 us -> 0 us
  between operations: 16.4 us -> 1.54 us
    reduce_scatter x4 -> x0, waiting for transfers between devices: 229 us -> none  [the longest x1 96.7 us: body(): lax.psum_scatter(jnp.einsum('rd,rf->df', columns, grad_pre, preferred_ele...]
    pallas_call x0 -> x1, Pallas kernels: none -> 203 us  [fast_body(): pl.pallas_call(functools.partial(layer_kernel, n_ep, seq), name='layer',...]
    dot_general x25 -> x0, matrix products: 114 us -> none  [the longest x1 14.9 us: body(): jnp.einsum('rd,fd->rf', grad_rows, w_out[0], preferred_element_type=jnp.f...]
    unnamed x135 -> x16, local copies, waits for them, and re-layouts: 41.7 us -> 4.49 us
    reshape x9 -> x0, local copies, waits for them, and re-layouts: 28 us -> none  [the longest x1 6.62 us: body(): qkv_heads = qkv_rows.reshape(slot_count, seq_len, 3, HEADS, HEAD_DIM)]
    psum x1 -> x0, waiting for transfers between devices: 23.1 us -> none  [body(): lax.psum(partial_sums[0].astype(jnp.bfloat16), 'dp').astype(jnp.float32)]
    psum x1 -> x0, blocking collectives: 22.1 us -> none  [body(): lax.psum(partial_sums[3].astype(jnp.bfloat16), 'dp').astype(jnp.float32)]
    all_to_all x4 -> x0, starting transfers between devices: 17.8 us -> none  [the longest x1 4.56 us: body(): lax.all_to_all(produced.reshape(inbox.shape), 'ep', split_axis=0, concat_...]
  transfers between devices with their start and end apart: 10 -> 0, of which waited for: 6 -> 0; matrix products, arithmetic and copies ran while one was open for 27% -> 0% of each run, Pallas kernels for 0% -> 0%
where the time goes in v1:
time: 225 us; the launch traced here: 222 us
  Pallas kernels  203 us (90%)
  local copies, waits for them, and re-layouts  11.5 us (5%)
  other arithmetic  5.23 us (2%)
    pallas_call x1, Pallas kernels, fast_body(): pl.pallas_call(functools.partial(layer_kernel, n_ep, seq), name='layer',...  203 us

profile of v1, /device:TPU:0, one launch (start us, length us, event | category | flops | bytes accessed | tf_op | source)
XLA Modules:
  0.0 221.5 jit_solution(6463385411159662452)
XLA Ops:
  1.3 0.7 stack.15
  2.0 0.7 stack.16
  2.7 0.7 stack.17
  3.4 0.7 stack.18
  4.1 0.6 pad_maximum_fusion.gains
  4.7 0.0 copy-start.2
  4.7 1.2 copy_select_fusion
  5.9 0.9 pad.8.gl
  6.8 0.0 copy-done.2
  6.8 0.1 copy.24
  6.9 0.9 pad.7.xb
  7.7 203.3 %layer.1 = (bf16[2,208,768]{2,1,0:T(8,128)(2,1)}, f32[2,208,768]{2,1,0:T(8,128)}, f32[8,192]{1,0:T(8,128)}, bf16[768,384]{1,0:T(8,128)(2,1)}, bf16[96,3072]{1,0:...) custom-call(s32[1]{0:T(128)} %copy.30.live, s32[2,2,197]{2,1,0:T(2,128)} %bitcast.18, ...), custom_call_target="tpu_custom_call" | custom-call | tf_op jit(solution)/shard_map/layer/pallas_call | solution.py:730
  211.0 0.0 copy-start.5
  211.1 0.0 copy-start.1
  211.1 1.2 slice.27
  212.3 1.3 copy.26
  213.6 0.0 copy-done.5
  213.6 0.6 slice_bitcast_fusion
  214.2 0.6 fusion
  214.7 0.0 copy-done.1
  214.8 0.9 slice_convert_fusion.1
  215.6 0.0 copy-start.4
  215.6 1.3 slice_convert_fusion
  216.9 0.0 copy-done.4
  216.9 1.1 bitcast_convert_fusion
  218.0 0.1 copy-done.3
  218.1 0.1 convert_bitcast_fusion
  218.2 0.0 copy-start
  218.2 1.4 copy.28
  219.6 0.0 copy-done
  219.6 0.1 slice.28
  219.7 1.6 copy.27
  (2 shorter events, 0.0 us)
Async XLA Ops:
  4.7 2.1 copy-start.2
  211.0 2.5 %copy-start.5 = (f32[8,192]{1,0:T(8,128)S(1)}, f32[8,192]{1,0:T(8,128)}, u32[]{:S(2)}) copy-start(f32[8,192]{1,0:T(8,128)} %get-tuple-element.19) | copy-start | bytes 18436
  211.1 3.7 %copy-start.1 = (bf16[192,3072]{1,0:T(8,128)(2,1)S(1)}, bf16[192,3072]{1,0:T(8,128)(2,1)}, u32[]{:S(2)}) copy-start(bf16[192,3072]{1,0:T(8,128)(2,1)} %get-tuple-element.20) | copy-start | bytes 3538948
  215.6 1.3 copy-start.4
  216.9 1.2 copy-start.3
  218.2 1.4 copy-start

commit v2 on v1

--- a/solution.py
+++ b/solution.py
@@ -58,9 +58,9 @@
 COPIES = {}
 for _name, _count in (
     ("uP", 2), ("uO", 2), ("uF", 2), ("sP", 1), ("sO", 1), ("sF", 1), ("gP", 2), ("gO", 2), ("gF", 2),
-    ("ox", 4), ("oz", 3), ("ix", 4), ("iz", 12),
+    ("ox", 4), ("oq", 2), ("oz", 1), ("oc", 2), ("ix", 4), ("iq", 8), ("iz", 4), ("ic", 8), ("jq", 2), ("jz", 1), ("jc", 2),
     ("dP", 2), ("dD", 2), ("dO", 2), ("eP", 1), ("eD", 1), ("eO", 1), ("yP", 2), ("yD", 2), ("yO", 2),
-    ("C", 8), ("Y", 4), ("X", 4), ("Z", 12), ("AZ", 12), ("AX", 4), ("mC", 2), ("mY", 1), ("mX", 1), ("mZ", 3),
+    ("C", 8), ("Y", 4), ("X", 4), ("R1", 4), ("R2", 4), ("R3", 4), ("AX", 4), ("mC", 2), ("mY", 1), ("mX", 1), ("mZ", 3),
 ):
     COPIES[_name] = sum(n for _, n in COPIES.values()), _count
 N_COPIES = sum(n for _, n in COPIES.values())
@@ -68,11 +68,11 @@
 
 def layer_kernel(
     experts, seq, live, routes, gains, wrt, xb, gl, w_in, w_out, wqkv, wo,
-    bo_o, DH, sm_o, wo_o, wi_o, sg_o, qa_h, c_h,
+    bo_o, DH, sm_o, wo_o, wi_o, sg_o, qa_h, c_h, u_h,
     U, G, SL, WR, WI, WO, M, D, X, GE, DT,
-    GOs, GOk, GOx, GOz, GIs, GIk, GIx, GIz,
+    GOs, GOk, GOx, GOz, GIs, GIk, GIx, GIz, GJ,
     H, LS, GD, RP, RD, RO, EP, ED, EO, ES, YP, YD, YO, SM, SMx,
-    ssem, rsem, lsem, free,
+    ssem, rsem, lsem, free, credit,
 ):
     f, width = WO.shape
     sp, rows, half_rows = 208, 416, 512
@@ -85,13 +85,19 @@
     to_x = {"dp": z * 2 + 1 - x}
     zs = [lax.rem(z + k, 4) for k in range(4)]
     to_z = [{"dp": zs[k] * 2 + x} for k in range(4)]
+    side = z // 2
+    mate, near, far = z + 1 - 2 * (z % 2), 2 - side, 3 - 3 * side
+    is_end = z % 2 == side
+    is_mid = z % 2 != side
+    to_mate, to_near, to_far = ({"dp": other * 2 + x} for other in (mate, near, far))
     friends = (to_p, to_o, to_x, to_z[1], to_z[2], to_z[3])
     g1, b1, g2, b2 = (gains[n:n + 1, :] for n in range(4))
 
-    def rc(name, i, src, dst, dev):
+    def rc(name, i, src, dst, dev, arrival=None):
         at = COPIES[name][0] + i
+        to = at if arrival is None else COPIES[name][0] + arrival
         return pltpu.make_async_remote_copy(
-            src_ref=src, dst_ref=dst, send_sem=ssem.at[at], recv_sem=rsem.at[at], device_id=dev, device_id_type=MESH)
+            src_ref=src, dst_ref=dst, send_sem=ssem.at[at], recv_sem=rsem.at[to], device_id=dev, device_id_type=MESH)
 
     def lc(i, src, dst):
         return pltpu.make_async_copy(src, dst, lsem.at[i])
@@ -149,18 +155,19 @@
             r0 = slice(i * sp, (i + 1) * sp)
             n1, _ = norm_parts(GE[r0, :].astype(F32))
             D[r0, 3 * width:] = (n1 * g1 + b1).astype(BF)
+    with sc("barrier"):
+        pl.semaphore_wait(barrier, 6)
+    sO.start()
+    sP.start()
+    for i in range(2):
+        load_g[i].wait()
+        gO[i].start()
+        gP[i].start()
     with sc("qkv"):
         for n in range(3):
             load_w[n].wait()
             D[0:rows, n * width:(n + 1) * width] = dot(
                 D[0:rows, 3 * width:], WO[n * width:(n + 1) * width, :]).astype(BF)
-    with sc("barrier"):
-        pl.semaphore_wait(barrier, 6)
-    sO.start()
-    sP.start()
-    load_g[0].wait()
-    gO[0].start()
-    gP[0].start()
     LS[...] = jnp.zeros(LS.shape, F32)
 
     def attend(i, per):
@@ -204,10 +211,8 @@
             U[0, i, :sp, :] = (n2 * g2 + b2).astype(BF)
         uO[i].start()
         uP[i].start()
-    load_g[1].wait()
-    gO[1].start()
-    gP[1].start()
     keep = [lc(0, D.at[pl.ds(0, rows)], qa_h), lc(1, D.at[pl.ds(rows, rows), pl.ds(0, width)], c_h)]
+    keep += [lc(3 + i, U.at[0, i, top], u_h.at[pl.ds(i * sp, sp)]) for i in range(2)]
     load_out = lc(2, w_out.at[0], WO)
     for cp in keep + [load_out]:
         cp.start()
@@ -225,25 +230,26 @@
     c0 = 0.7978845608028654
     c1 = c0 * 0.044715
 
-    def expert_in(first):
-        rs = slice(first, first + half_rows)
-
-        def step(n, carry):
-            cols = pl.ds(pl.multiple_of(n * tile, tile), tile)
-            v = dot(X[rs, :], WI[:, cols])
-            w = v * v
-            t = jnp.tanh(v * (c0 + c1 * w))
-            h = 0.5 + 0.5 * t
-            M[rs, cols] = (v * h).astype(BF)
-            D[rs, cols] = (h + h * (1.0 - t) * (v * (c0 + 3.0 * c1 * w))).astype(BF)
-            return carry
-
-        lax.fori_loop(0, tiles, step, 0)
+    def hidden(rs, cols):
+        v = dot(X[rs, :], WI[:, cols])
+        w = v * v
+        t = jnp.tanh(v * (c0 + c1 * w))
+        h = 0.5 + 0.5 * t
+        M[rs, cols] = (v * h).astype(BF)
+        D[rs, cols] = (h + h * (1.0 - t) * (v * (c0 + 3.0 * c1 * w))).astype(BF)
+
+    def gate(rs):
         r = dot_nt(X[rs, :], WR[...])
         r = jnp.where(lane(r.shape) < experts, r, NEG)
         r = jnp.exp(r - jnp.max(r, axis=-1, keepdims=True))
         r = r / jnp.sum(r, axis=-1, keepdims=True)
         GD[rs, 0:1] = jnp.sum(jnp.where(lane(r.shape) == ep, r, 0.0), axis=-1, keepdims=True)
+
+    first_half, second_half = slice(0, half_rows), slice(half_rows, 2 * half_rows)
+
+    def first_in(n, carry):
+        hidden(first_half, pl.ds(pl.multiple_of(n * tile, tile), tile))
+        return carry
 
     def gather_grads(s):
         rs = slice(s * LP, (s + 1) * LP)
@@ -261,12 +267,18 @@
         for cp in keep:
             cp.wait()
     with sc("expert_in_0"):
-        expert_in(0)
-    with sc("wait_g0"):
+        gate(first_half)
+        lax.fori_loop(0, tiles, first_in, 0)
+    with sc("wait_gO"):
         sO.wait_recv()
         sF.start()
-        gO[0].wait_recv()
-        gF[0].start()
+        for i in range(2):
+            gO[i].wait_recv()
+            gF[i].start()
+        for i in range(2):
+            gP[i].wait_recv()
+        gather_grads(0)
+        gather_grads(1)
     with sc("wait_uO"):
         for i in range(2):
             uO[i].wait_recv()
@@ -277,18 +289,9 @@
         for i in range(2):
             uF[i].wait_recv()
         gather(3)
-    with sc("expert_in_1"):
-        expert_in(half_rows)
-    with sc("wait_gP"):
-        for i in range(2):
-            gP[i].wait_recv()
-        gather_grads(0)
-        gather_grads(1)
-    with sc("wait_gO"):
-        gO[1].wait_recv()
-        gF[1].start()
+        gate(second_half)
+    with sc("wait_gF"):
         gather_grads(2)
-    with sc("wait_gF"):
         for i in range(2):
             gF[i].wait_recv()
         gather_grads(3)
@@ -296,18 +299,43 @@
     def ox(t):
         return rc("ox", t, GOs.at[t], GOx.at[t], to_x)
 
-    def oz(k):
-        return rc("oz", k - 1, GOk.at[k - 1], GOz.at[k - 1], to_z[k])
-
     def ix(j):
         return rc("ix", j, GIs.at[j], GIx.at[j], to_x)
 
-    def iz(j, k):
-        return rc("iz", j * 3 + k - 1, GIk.at[j, zs[k]], GIz.at[k - 1, j], to_z[k])
+    def oq(t):
+        return rc("oq", t, GOk.at[t], DT.at[:, pl.ds(t * (width // 2), width // 2)], to_mate)
+
+    oz = rc("oz", 0, GOk.at[2], GOz.at[0], to_mate)
+    oc = [rc("oc", t, GOk.at[t], GOz.at[1], dev, 0) for t, dev in enumerate((to_far, to_near))]
+
+    def iq(j, t):
+        return rc("iq", j * 2 + t, GIk.at[j, (far, near)[t]], GJ.at[t] if j == 0 else
+                  DT.at[pl.ds((j * 2 + t) * (width // 8), width // 8), pl.ds(0, width)], to_mate)
+
+    def jq(t):
+        return rc("jq", t, GIs.at[0, (far, near)[t]], GJ.at[2 + t], to_mate)
+
+    jz = rc("jz", 0, GIs.at[0, mate], GIx.at[0, 0], to_mate)
+
+    def jc(t):
+        return rc("jc", t, GIs.at[0, (far, near)[t]], GIx.at[0, 1], (to_far, to_near)[t], 0)
+
+    ix0 = rc("ix", 0, GIs.at[0, z], GIx.at[0, 2], to_x)
+
+    def iz(j):
+        return rc("iz", j, GIk.at[j, mate], GIz.at[0, j], to_mate)
+
+    def ic(j, t):
+        return rc("ic", j * 2 + t, GIk.at[j, (far, near)[t]], GIz.at[1, j], (to_far, to_near)[t], j * 2)
 
     def w_out_tile(t, carry):
-        zp = lax.rem(z + 1 + t, 4)
-        r = dot(DT[...], M[:, pl.ds(pl.multiple_of(zp * width, width), width)])
+        is0, is3 = (3 - t) // 3, t // 3
+        is2 = t // 2 - is3
+        zp = is0 * far + (1 - is0 - is2 - is3) * near + is2 * mate + is3 * z
+        cols = pl.ds(pl.multiple_of(zp * width, width), width)
+        for piece in range(3):
+            hidden(second_half, pl.ds(pl.multiple_of(zp * width + piece * 256, 256), 256))
+        r = dot(DT[...], M[:, cols])
         lo, hi = r[:, :width // 2], r[:, width // 2:]
         GOs[t] = jnp.where(x == 0, hi, lo).astype(BF)
         GOk[t] = jnp.where(x == 0, lo, hi).astype(BF)
@@ -316,20 +344,76 @@
 
     with sc("w_out_tiles"):
         lax.fori_loop(0, 4, w_out_tile, 0)
+    pl.semaphore_signal(credit.at[0], inc=1, device_id=to_mate, device_id_type=MESH)
 
     def take_o(t):
         with sc("take_o%d" % t):
             ox(t).wait_recv()
             GOk[t] = (GOk[t].astype(F32) + GOx[t].astype(F32)).astype(BF)
-            if t < 3:
-                oz(t + 1).start()
+            if t == 0:
+                pl.semaphore_wait(credit.at[0], 1)
+            if t < 2:
+                @pl.when(is_end)
+                def _():
+                    oq(t).start()
+            if t == 2:
+                oz.start()
+
+    def pass_o(t):
+        with sc("pass_o%d" % t):
+            @pl.when(is_mid)
+            def _():
+                oq(t).wait_recv()
+                GOk[t] = (GOk[t].astype(F32) + DT[:, t * (width // 2):(t + 1) * (width // 2)].astype(F32)).astype(BF)
+                oc[t].start()
+            if t == 1:
+                pl.semaphore_signal(credit.at[1], inc=1, device_id=to_mate, device_id_type=MESH)
 
     def take_i(j):
         with sc("take_i%d" % j):
-            ix(j).wait_recv()
-            GIk[j] = (GIk[j].astype(F32) + GIx[j].astype(F32)).astype(BF)
-            for k in range(1, 4):
-                iz(j, k).start()
+            if j > 0:
+                ix(j).wait_recv()
+                GIk[j] = (GIk[j].astype(F32) + GIx[j].astype(F32)).astype(BF)
+            if j == 1:
+                pl.semaphore_wait(credit.at[1], 1)
+
+            @pl.when(is_end)
+            def _():
+                for t in range(2):
+                    iq(j, t).start()
+                    if j == 0:
+                        jq(t).start()
+
+            iz(j).start()
+            if j == 0:
+                jz.start()
+
+    def pass_i(j):
+        with sc("pass_i%d" % j):
+            @pl.when(is_mid)
+            def _():
+                for t in range(2):
+                    at = (far, near)[t]
+                    iq(j, t).wait_recv()
+                    if j == 0:
+                        came = GJ[t]
+                    else:
+                        r0 = (j * 2 + t) * (width // 8)
+                        came = DT[r0:r0 + width // 8, 0:width]
+                    GIk[j, at] = (GIk[j, at].astype(F32) + came.astype(F32)).astype(BF)
+                    ic(j, t).start()
+                    if j == 0:
+                        jq(t).wait_recv()
+                        GIs[0, at] = (GIs[0, at].astype(F32) + GJ[2 + t].astype(F32)).astype(BF)
+                        jc(t).start()
+
+    def cross_first():
+        with sc("cross_first"):
+            jz.wait_recv()
+            rc("jc", 0, GIs.at[0, far], GIx.at[0, 1], to_far, 0).wait_recv()
+            total = GIs[0, z].astype(F32) + GIx[0, 0].astype(F32) + GIx[0, 1].astype(F32)
+            GIs[0, z] = total.astype(BF)
+            ix0.start()
 
     load_out.wait()
     GD[:, 1:2] = jnp.zeros((GD.shape[0], 1), F32)
@@ -344,8 +428,10 @@
         return carry
 
     with sc("expert_back"):
-        lax.fori_loop(0, tiles, expert_back, 0)
+        lax.fori_loop(0, tiles // 2, expert_back, 0)
     take_o(0)
+    with sc("expert_back"):
+        lax.fori_loop(tiles // 2, tiles, expert_back, 0)
 
     dP = [rc("dP", i, U.at[1, i, top], RP.at[i], to_p) for i in range(2)]
     dD = [rc("dD", i, U.at[3, i, top], RD.at[i], to_p) for i in range(2)]
@@ -363,28 +449,32 @@
     def scatter(s, values):
         return dot_tn(onehot(s), values)
 
-    for s in (3, 2, 1, 0):
-        with sc("du%d" % s):
-            rs = slice(s * LP, (s + 1) * LP)
-            out = scatter(s, dot_nt(D[rs, :], WI[...]).astype(BF))
-            if s == 0:
-                for i in range(2):
-                    DH[i] = out[i * LP:i * LP + sp]
-            else:
-                U[s] = out.astype(BF).reshape(2, LP, width)
-            dg = GD[rs, 1:2]
-            hi = dg.astype(BF)
-            rest = (dg - hi.astype(F32)).astype(BF)
-            at = lane((LP, 128))
-            zero = jnp.zeros((LP, 128), BF)
-            two = jnp.where(at == ep, hi, zero) + jnp.where(at == ep + 64, rest, zero)
-            ES[s] = scatter(s, two).astype(BF).reshape(2, LP, 128)
-            if s == 3:
-                for cp in dD + [eD]:
-                    cp.start()
-            if s == 1:
-                for cp in dP + [eP]:
-                    cp.start()
+    def back_rows(step, carry):
+        s = 3 - step
+        rs = pl.ds(pl.multiple_of(s * LP, LP), LP)
+        U[s] = scatter(s, dot_nt(D[rs, :], WI[...]).astype(BF)).astype(BF).reshape(2, LP, width)
+        dg = GD[rs, 1:2]
+        hi = dg.astype(BF)
+        rest = (dg - hi.astype(F32)).astype(BF)
+        at = lane((LP, 128))
+        zero = jnp.zeros((LP, 128), BF)
+        two = jnp.where(at == ep, hi, zero) + jnp.where(at == ep + 64, rest, zero)
+        ES[s] = scatter(s, two).astype(BF).reshape(2, LP, 128)
+
+        @pl.when(step == 0)
+        def _():
+            for cp in dD + [eD]:
+                cp.start()
+
+        @pl.when(step == 2)
+        def _():
+            for cp in dP + [eP]:
+                cp.start()
+
+        return carry
+
+    with sc("du"):
+        lax.fori_loop(0, 4, back_rows, 0)
     with sc("combine_du"):
         for i in range(2):
             dD[i].wait_recv()
@@ -393,6 +483,7 @@
         eD.wait_recv()
         ES[2] = ES[2] + ED[...]
         eO.start()
+    pass_o(0)
     take_o(1)
 
     def w_in_tile(j, carry):
@@ -400,34 +491,49 @@
         first, second = r[:, 0], r[:, 1]
         GIs[j] = jnp.where(x == 0, second, first).astype(BF)
         GIk[j] = jnp.where(x == 0, first, second).astype(BF)
-        ix(j).start()
+
+        @pl.when(j > 0)
+        def _():
+            ix(j).start()
+
         return carry
 
     with sc("w_in_tiles"):
         lax.fori_loop(0, 4, w_in_tile, 0)
+    take_i(0)
     for dev in friends:
         pl.semaphore_signal(free, inc=1, device_id=dev, device_id_type=MESH)
 
     for cp in gP + gO + gF:
         cp.wait_send()
-    for s in (3, 2, 1, 0):
-        with sc("o%d" % s):
-            rs = slice(s * LP, (s + 1) * LP)
-            o = dot(M[rs, :], WO[...]).astype(BF).astype(F32)
-            out = scatter(s, (GD[rs, 0:1] * o).astype(BF)).astype(BF)
-            if s == 0:
-                X[0:half_rows, :] = out
-            else:
-                G[s] = out.reshape(2, LP, width)
-            if s == 3:
-                for cp in yD:
-                    cp.start()
-            if s == 1:
-                for cp in yP:
-                    cp.start()
+    for i in range(2):
+        X[half_rows + i * sp:half_rows + (i + 1) * sp, :] = G[0, i, :sp, :]
+
+    def out_rows(step, carry):
+        s = 3 - step
+        rs = pl.ds(pl.multiple_of(s * LP, LP), LP)
+        o = dot(M[rs, :], WO[...]).astype(BF).astype(F32)
+        G[s] = scatter(s, (GD[rs, 0:1] * o).astype(BF)).astype(BF).reshape(2, LP, width)
+
+        @pl.when(step == 0)
+        def _():
+            for cp in yD:
+                cp.start()
+
+        @pl.when(step == 2)
+        def _():
+            for cp in yP:
+                cp.start()
+
+        return carry
+
+    with sc("o"):
+        lax.fori_loop(0, 4, out_rows, 0)
+    pass_o(1)
     late = attention_weights(3) + [
         lc(7, qa_h, M.at[pl.ds(0, rows)]), lc(8, c_h, M.at[pl.ds(rows, rows), pl.ds(0, width)])
     ] + [lc(9 + i, xb.at[i], GE.at[pl.ds(rows + i * sp, sp)]) for i in range(2)]
+    late.append(lc(11, u_h, M.at[pl.ds(rows, rows), pl.ds(width, width)]))
     for cp in late:
         cp.start()
     with sc("combine_y"):
@@ -436,6 +542,8 @@
             G[2, i, :sp, :] = (G[2, i, :sp, :].astype(F32) + YD[i].astype(F32)).astype(BF)
             yO[i].start()
     take_o(2)
+    for cp in late:
+        cp.wait()
 
     with sc("wait_du"):
         for i in range(2):
@@ -448,10 +556,10 @@
         gain2 = jnp.zeros((1, width), F32)
         bias2 = jnp.zeros((1, width), F32)
         for i in range(2):
-            du = DH[i] + RP[i].astype(F32) + RO[i].astype(F32)
+            du = U[0, i, :sp, :].astype(F32) + RP[i].astype(F32) + RO[i].astype(F32)
             back = ES[0, i, :sp, :].astype(F32) + EP[i, :sp, :].astype(F32) + EO[i, :sp, :].astype(F32)
             back = back + pltpu.roll(back, 64, axis=1)
-            own = U[0, i, :sp, :]
+            own = M[rows + i * sp:rows + (i + 1) * sp, width:2 * width]
             r = dot_nt(own, WR[...])
             r = jnp.where(lane(r.shape) < experts, r, NEG)
             r = jnp.exp(r - jnp.max(r, axis=-1, keepdims=True))
@@ -462,22 +570,15 @@
             n2, inv2 = norm_parts(H[i])
             gain2 = gain2 + jnp.sum(du * n2, axis=0, keepdims=True)
             bias2 = bias2 + jnp.sum(du, axis=0, keepdims=True)
-            dh = G[0, i, :sp, :].astype(F32) + norm_backward(du * g2, n2, inv2)
+            on = (live[0] > i).astype(F32)
+            dh = X[half_rows + i * sp:half_rows + (i + 1) * sp, :].astype(F32) * on + norm_backward(du * g2, n2, inv2)
             DH[i] = dh
             GE[i * sp:(i + 1) * sp, :] = dh.astype(BF)
         SM[...] = router.astype(BF)
-    for cp in late:
-        cp.wait()
 
     def part(e, b):
         return pl.ds(pl.multiple_of(e * shard, shard), shard), pl.ds(b * width, width)
 
-    def mine(b, h):
-        return pl.ds(pl.multiple_of(b * width + h * (width // 2), 128), width // 2)
-
-    def rest(r0, n, b, second):
-        return D.at[r0:r0 + n, pl.ds(b * width + second * (width // 2), width // 2)]
-
     def cp_c(b, i):
         return rc("C", b * 2 + i, WI.at[part(i * 2 + 1 - core, b)], D.at[pl.ds(i * shard, shard), pl.ds(b * width, width)], to_p)
 
@@ -487,22 +588,26 @@
     def own_rows(k=0, n=shard):
         return pl.ds(pl.multiple_of(ep * shard + k * block, block), n)
 
+    def half(b, h):
+        return pl.ds(pl.multiple_of(b * width + h * (width // 2), 128), width // 2)
+
+    def rest(quarter, b, second):
+        return D.at[pl.ds(quarter * shard, shard), pl.ds(b * width + second * (width // 2), width // 2)]
+
     def cp_x(b):
-        return rc("X", b, WI.at[own_rows(), mine(b, 1 - x)], rest(3 * shard, shard, b, 0), to_x)
-
-    def cp_z(b, k):
-        return rc("Z", b * 3 + k - 1, WI.at[own_rows(zs[k], block), mine(b, x)],
-                  rest(4 * shard + (k - 1) * block, block, b, 0), to_z[k])
-
-    def result(k, b):
-        return D.at[pl.ds(pl.multiple_of(4 * shard + k * block, block), block),
-                    pl.ds(b * width + width // 2, width // 2)]
-
-    def cp_az(b, k):
-        return rc("AZ", b * 3 + k - 1, result(z, b), result(z, b), to_z[k])
+        return rc("X", b, WI.at[own_rows(), half(b, 1 - x)], rest(3, b, 0), to_x)
+
+    def cp_r1(b):
+        return rc("R1", b, WI.at[own_rows(), half(b, x)], rest(4, b, 0), to_mate)
+
+    def cp_r2(b):
+        return rc("R2", b, WI.at[own_rows(), half(b, x)], rest(4, b, 1), to_near)
+
+    def cp_r3(b):
+        return rc("R3", b, rest(0, b, 0), rest(0, b, 0), to_mate)
 
     def cp_ax(b):
-        return rc("AX", b, rest(4 * shard, shard, b, 1), rest(3 * shard, shard, b, 1), to_x)
+        return rc("AX", b, rest(0, b, 0), rest(1, b, 0), to_x)
 
     def stage_c(b):
         for i in range(2):
@@ -524,29 +629,40 @@
             WI[at] = (WI[at].astype(F32) + D[2 * shard:3 * shard, b * width:(b + 1) * width].astype(F32)).astype(BF)
             cp_x(b).start()
 
-    def stage_z(b):
-        with sc("stage_z%d" % b):
+    def add_own(b, came):
+        at = own_rows(), half(b, x)
+        WI[at] = (WI[at].astype(F32) + came[...].astype(F32)).astype(BF)
+
+    def stage_r1(b):
+        with sc("stage_r1_%d" % b):
             cp_x(b).wait_recv()
-            at = own_rows(), mine(b, x)
-            WI[at] = (WI[at].astype(F32) + rest(3 * shard, shard, b, 0)[...].astype(F32)).astype(BF)
-            for k in range(1, 4):
-                cp_z(b, k).start()
-
-    def stage_az(b):
-        with sc("stage_az%d" % b):
-            for k in range(1, 4):
-                cp_z(b, k).wait_recv()
-            total = WI[own_rows(z, block), mine(b, x)].astype(F32)
-            for k in range(3):
-                total = total + rest(4 * shard + k * block, block, b, 0)[...].astype(F32)
-            result(z, b)[...] = total.astype(BF)
-            for k in range(1, 4):
-                cp_az(b, k).start()
-
-    def stage_ax(b):
-        with sc("stage_ax%d" % b):
-            for k in range(1, 4):
-                rc("AZ", b * 3 + k - 1, result(zs[4 - k], b), result(zs[4 - k], b), to_z[k]).wait_recv()
+            add_own(b, rest(3, b, 0))
+
+            @pl.when(is_end)
+            def _():
+                cp_r1(b).start()
+
+    def stage_r2(b):
+        with sc("stage_r2_%d" % b):
+            @pl.when(is_mid)
+            def _():
+                cp_r1(b).wait_recv()
+                add_own(b, rest(4, b, 0))
+                cp_r2(b).start()
+
+    def stage_r3(b):
+        with sc("stage_r3_%d" % b):
+            @pl.when(is_mid)
+            def _():
+                cp_r2(b).wait_recv()
+                total = WI[own_rows(), half(b, x)].astype(F32) + rest(4, b, 1)[...].astype(F32)
+                rest(0, b, 0)[...] = total.astype(BF)
+                cp_r3(b).start()
+
+            @pl.when(is_end)
+            def _():
+                cp_r3(b).wait_recv()
+
             cp_ax(b).start()
 
     with sc("attn_out_grads"):
@@ -555,7 +671,6 @@
     with sc("wait_free"):
         pl.semaphore_wait(free, 6)
     stage_c(3)
-    take_o(3)
 
     def pair_back(h, carry):
         def cols(n):
@@ -584,7 +699,8 @@
     with sc("attention_back_a"):
         lax.fori_loop(0, width // 256, pair_back, 0)
     stage_y(3)
-    take_i(0)
+    pass_i(0)
+    take_o(3)
     with sc("attention_back_b"):
         lax.fori_loop(width // 256, width // 128, pair_back, 0)
     for n in range(3):
@@ -593,6 +709,7 @@
             WI[:, n * width:(n + 1) * width] = dot_tn(M[0:rows, 3 * width:], grads).astype(BF)
         stage_c(n)
     stage_x(3)
+    take_i(1)
     with sc("ln1_back"):
         gain1 = jnp.zeros((1, width), F32)
         bias1 = jnp.zeros((1, width), F32)
@@ -631,82 +748,105 @@
             yP[i].wait_recv()
             yO[i].wait_recv()
             on = (live[0] > i).astype(F32)
-            mix = X[i * LP:i * LP + sp, :].astype(F32) + YP[i].astype(F32) + YO[i].astype(F32)
+            mix = G[0, i, :sp, :].astype(F32) + YP[i].astype(F32) + YO[i].astype(F32)
             bo_o[i] = ((H[i] + mix) * on).astype(BF)
-    take_i(1)
+    cross_first()
+    with sc("o_sum"):
+        oz.wait_recv()
+        rc("oc", 0, GOk.at[0], GOz.at[1], to_far, 0).wait_recv()
+        total = GOk[3].astype(F32) + GOz[0].astype(F32) + GOz[1].astype(F32)
+        GOk[3] = total.astype(BF)
+        outs = [lc(0, GOk.at[3], wo_o)]
+        outs[0].start()
+    pass_i(1)
+    take_i(2)
     stage_x(0)
-    take_i(2)
+    pass_i(2)
     stage_x(1)
-    stage_z(3)
+    take_i(3)
     stage_x(2)
     with sc("small_x"):
         mY.wait_recv()
         at = small(ep)
         SM[at, :] = (SM[at, :].astype(F32) + SMx[2].astype(F32)).astype(BF)
         mX.start()
-    take_i(3)
+    stage_r1(3)
+    stage_r1(0)
+    pass_i(3)
+    stage_r2(3)
+    stage_r1(1)
+    stage_r2(0)
+    stage_r1(2)
+    stage_r2(1)
+    stage_r3(3)
+    stage_r2(2)
+    stage_r3(0)
     with sc("small_z"):
         mX.wait_recv()
         SMx[3] = (SM[small(ep), :].astype(F32) + SMx[3].astype(F32)).astype(BF)
         for cp in mZ:
             cp.start()
-    stage_az(3)
-    for b in range(3):
-        stage_z(b)
-    stage_ax(3)
-    for b in range(3):
-        stage_az(b)
-    with sc("o_sum"):
-        for k in range(1, 4):
-            oz(k).wait_recv()
-        total = GOk[3].astype(F32)
-        for k in range(3):
-            total = total + GOz[k].astype(F32)
-        GOk[3] = total.astype(BF)
-        outs = [lc(0, GOk.at[3], wo_o)]
-        outs[0].start()
+    stage_r3(1)
+    stage_r3(2)
     for j in range(4):
-        with sc("i_sum"):
-            for k in range(1, 4):
-                iz(j, k).wait_recv()
-            total = GIk[j, z].astype(F32)
-            for k in range(3):
-                total = total + GIz[k, j].astype(F32)
-            GIx[j, 0] = total.astype(BF)
-            outs.append(lc(1 + j, GIx.at[j, 0], wi_o.at[:, pl.ds(j * width, width)]))
+        with sc("i_sum%d" % j):
+            iz(j).wait_recv()
+            ic(j, 0).wait_recv()
+            total = GIk[j, z].astype(F32) + GIz[0, j].astype(F32) + GIz[1, j].astype(F32)
+            if j == 0:
+                ix0.wait_recv()
+                total = total + GIx[0, 2].astype(F32)
+            GIx[j, 3] = total.astype(BF)
+            outs.append(lc(1 + j, GIx.at[j, 3], wi_o.at[:, pl.ds(j * width, width)]))
             outs[-1].start()
     with sc("small_sum"):
         for cp in mZ:
             cp.wait_recv()
         total = SMx[3].astype(F32) + SMx[4].astype(F32) + SMx[5].astype(F32) + SMx[6].astype(F32)
         sm_o[...] = jnp.transpose(total)[0:8, :]
-    for b in range(3):
-        stage_ax(b)
     for b in (3, 0, 1, 2):
-        outs.append(lc(5 + b, rest(4 * shard, shard, b, 1), sg_o.at[:, mine(b, x)]))
-        outs[-1].start()
-    with sc("wait_ax"):
-        for b in (3, 0, 1, 2):
+        with sc("wait_ax"):
             cp_ax(b).wait_recv()
-            outs.append(lc(9 + b, rest(3 * shard, shard, b, 1), sg_o.at[:, mine(b, 1 - x)]))
+            outs.append(lc(5 + b, rest(0, b, 0), sg_o.at[:, half(b, x)]))
+            outs[-1].start()
+            outs.append(lc(9 + b, rest(1, b, 0), sg_o.at[:, half(b, 1 - x)]))
             outs[-1].start()
     with sc("drain"):
         for cp in dP + dD + dO + yP + yD + yO + [sP, sO, sF, eP, eD, eO, mY, mX] + mC + mZ:
             cp.wait_send()
         for t in range(4):
             ox(t).wait_send()
-            ix(t).wait_send()
+            (ix(t) if t else ix0).wait_send()
+            iz(t).wait_send()
             cp_y(t).wait_send()
             cp_x(t).wait_send()
             cp_ax(t).wait_send()
             for i in range(2):
                 cp_c(t, i).wait_send()
-            for k in range(1, 4):
-                iz(t, k).wait_send()
-                cp_z(t, k).wait_send()
-                cp_az(t, k).wait_send()
-        for k in range(1, 4):
-            oz(k).wait_send()
+        oz.wait_send()
+        jz.wait_send()
+
+        @pl.when(is_end)
+        def _():
+            for t in range(4):
+                cp_r1(t).wait_send()
+            for t in range(2):
+                oq(t).wait_send()
+                jq(t).wait_send()
+                for j in range(4):
+                    iq(j, t).wait_send()
+
+        @pl.when(is_mid)
+        def _():
+            for t in range(4):
+                cp_r2(t).wait_send()
+                cp_r3(t).wait_send()
+            for t in range(2):
+                oc[t].wait_send()
+                jc(t).wait_send()
+                for j in range(4):
+                    ic(j, t).wait_send()
+
         for cp in outs:
             cp.wait()
 
@@ -717,8 +857,7 @@
     f = w_in.shape[2]
     cap = n_ep * LP
     pads = ((0, 0), (0, sp - seq), (0, 0))
-    on = (jnp.arange(slots, dtype=jnp.int32) < live[0])[:, None, None]
-    gl = jnp.pad(jnp.where(on, cot, jnp.zeros_like(cot)), pads)
+    gl = jnp.pad(cot, pads)
     xb = jnp.pad(tokens, pads)
     gains = jnp.stack([g1, b1, g2, b2])
     sds = jax.ShapeDtypeStruct
@@ -727,28 +866,28 @@
     b = lambda *shape: pltpu.VMEM(shape, BF)
     g = lambda *shape: pltpu.VMEM(shape, F32)
     shard = width // n_ep
-    bo, gt, sm, wo_t, wi, sg, _, _ = pl.pallas_call(
+    bo, gt, sm, wo_t, wi, sg, _, _, _ = pl.pallas_call(
         functools.partial(layer_kernel, n_ep, seq),
         name="layer",
         out_shape=(
             sds((slots, sp, width), BF), sds((slots, sp, width), F32), sds((8, shard), F32),
             sds((width, f // 8), BF), sds((width // 8, f), BF), sds((shard, 4 * width), BF),
-            sds((2 * sp, 4 * width), BF), sds((2 * sp, width), BF),
+            sds((2 * sp, 4 * width), BF), sds((2 * sp, width), BF), sds((2 * sp, width), BF),
         ),
         in_specs=[pl.BlockSpec(memory_space=pltpu.SMEM)] + [vm] * 3 + [anys] * 6,
-        out_specs=[vm] * 3 + [anys] * 5,
+        out_specs=[vm] * 3 + [anys] * 6,
         scratch_shapes=[
             b(4, 2, LP, width), b(4, 2, LP, width), g(4, 2, 8, LP), b(128, width), b(width, f), b(f, width),
             b(cap, f), b(cap, f), b(cap, width), b(cap, width), b(width, cap),
-            b(4, width, f // 8), b(4, width, f // 8), b(4, width, f // 8), b(3, width, f // 8),
+            b(4, width, f // 8), b(4, width, f // 8), b(4, width, f // 8), b(2, width, f // 8),
             b(4, 4, width // 8, width), b(4, 4, width // 8, width), b(4, 4, width // 8, width),
-            b(3, 4, width // 8, width),
+            b(2, 4, width // 8, width), b(4, width // 8, width),
             g(slots, sp, width), g(slots, sp, 128), g(cap, 2),
             b(2, sp, width), b(2, sp, width), b(2, sp, width),
             b(2, LP, 128), b(2, LP, 128), b(2, LP, 128), b(4, 2, LP, 128),
             b(2, sp, width), b(2, sp, width), b(2, sp, width), b(width, 128), b(7, shard, 128),
             pltpu.SemaphoreType.DMA((N_COPIES,)), pltpu.SemaphoreType.DMA((N_COPIES,)),
-            pltpu.SemaphoreType.DMA((14,)), pltpu.SemaphoreType.REGULAR,
+            pltpu.SemaphoreType.DMA((14,)), pltpu.SemaphoreType.REGULAR, pltpu.SemaphoreType.REGULAR((2,)),
         ],
         compiler_params=pltpu.CompilerParams(
             collective_id=0, has_side_effects=True, vmem_limit_bytes=67043328),

time: 225 us -> 203 us (0.902)
  Pallas kernels: 203 us -> 182 us
    pallas_call x1, Pallas kernels: 203 us -> 182 us  [fast_body(): pl.pallas_call(functools.partial(layer_kernel, n_ep, seq), name='layer',...]
    unnamed x16 -> x17, local copies, waits for them, and re-layouts: 4.49 us -> 5.69 us
where the time goes in v2:
time: 203 us; the launch traced here: 200 us
  Pallas kernels  182 us (90%)
  local copies, waits for them, and re-layouts  12.7 us (6%)
  other arithmetic  3.98 us (2%)
    pallas_call x1, Pallas kernels, fast_body(): pl.pallas_call(functools.partial(layer_kernel, n_ep, seq), name='layer',...  182 us
    unnamed x17, local copies, waits for them, and re-layouts  5.69 us

profile of v2, /device:TPU:0, one launch (start us, length us, event | category | flops | bytes accessed | tf_op | source)
XLA Modules:
  0.0 200.2 jit_solution(1632651900366602884)
XLA Ops:
  1.3 0.7 stack.15
  2.0 0.7 stack.16
  2.7 0.7 stack.17
  3.4 0.7 stack.18
  4.0 0.6 pad_maximum_fusion.gains
  4.7 0.0 copy-start.2
  4.7 1.2 copy.24
  5.9 0.9 pad.7.xb
  6.7 0.0 copy-done.2
  6.7 0.1 copy.25
  6.8 0.9 pad.8.gl
  7.7 181.8 %layer.1 = (bf16[2,208,768]{2,1,0:T(8,128)(2,1)}, f32[2,208,768]{2,1,0:T(8,128)}, f32[8,192]{1,0:T(8,128)}, bf16[768,384]{1,0:T(8,128)(2,1)}, bf16[96,3072]{1,0:...) custom-call(s32[1]{0:T(128)S(6)} %copy.29.live, ...), custom_call_target="tpu_custom_call" | custom-call | tf_op jit(solution)/shard_map/layer/pallas_call | solution.py:869
  189.5 0.0 copy-start.5
  189.5 0.0 copy-start.1
  189.5 1.2 slice.27
  190.7 1.3 copy.26
  192.0 0.0 copy-done.5
  192.0 0.6 slice_bitcast_fusion
  192.6 0.6 fusion
  193.2 0.0 copy-done.1
  193.2 0.9 slice_convert_fusion.1
  194.0 0.0 copy-start.4
  194.0 1.3 slice_convert_fusion
  195.4 0.0 copy-done.4
  195.4 1.1 bitcast_convert_fusion
  196.5 0.1 copy-done.3
  196.6 0.1 convert_bitcast_fusion
  196.6 0.0 copy-start
  196.7 1.4 copy.28
  198.0 0.0 copy-done
  198.0 0.1 slice.28
  198.1 1.6 copy.27
  (1 shorter events, 0.0 us)
Async XLA Ops:
  4.7 2.1 %copy-start.2 = (bf16[2,197,768]{2,0,1:T(2,128)(2,1)S(1)}, bf16[2,197,768]{2,0,1:T(2,128)(2,1)}, u32[]{:S(2)}) copy-start(bf16[2,197,768]{2,0,1:T(2,128)(2,1)} %param.25) | copy-start | bytes 1815556
  189.5 2.5 %copy-start.5 = (f32[8,192]{1,0:T(8,128)S(1)}, f32[8,192]{1,0:T(8,128)}, u32[]{:S(2)}) copy-start(f32[8,192]{1,0:T(8,128)} %get-tuple-element.19) | copy-start | bytes 18436
  189.5 3.7 %copy-start.1 = (bf16[192,3072]{1,0:T(8,128)(2,1)S(1)}, bf16[192,3072]{1,0:T(8,128)(2,1)}, u32[]{:S(2)}) copy-start(bf16[192,3072]{1,0:T(8,128)(2,1)} %get-tuple-element.20) | copy-start | bytes 3538948
  194.0 1.3 copy-start.4
  195.4 1.2 copy-start.3
  196.6 1.4 copy-start

commit v3 on v2

--- a/solution.py
+++ b/solution.py
@@ -67,7 +67,7 @@
 
 
 def layer_kernel(
-    experts, seq, live, routes, gains, wrt, xb, gl, w_in, w_out, wqkv, wo,
+    experts, seq, live, routes, g1, b1, g2, b2, wrt, xb, gl, w_in, w_out, wqkv, wo,
     bo_o, DH, sm_o, wo_o, wi_o, sg_o, qa_h, c_h, u_h,
     U, G, SL, WR, WI, WO, M, D, X, GE, DT,
     GOs, GOk, GOx, GOz, GIs, GIk, GIx, GIz, GJ,
@@ -91,7 +91,7 @@
     is_mid = z % 2 != side
     to_mate, to_near, to_far = ({"dp": other * 2 + x} for other in (mate, near, far))
     friends = (to_p, to_o, to_x, to_z[1], to_z[2], to_z[3])
-    g1, b1, g2, b2 = (gains[n:n + 1, :] for n in range(4))
+    g1, b1, g2, b2 = (v[...].reshape(1, width) for v in (g1, b1, g2, b2))
 
     def rc(name, i, src, dst, dev, arrival=None):
         at = COPIES[name][0] + i
@@ -102,7 +102,7 @@
     def lc(i, src, dst):
         return pltpu.make_async_copy(src, dst, lsem.at[i])
 
-    top = pl.ds(0, sp)
+    top, sent = pl.ds(0, sp), pl.ds(0, (seq + 7) // 8 * 8)
     barrier = pltpu.get_barrier_semaphore()
     for dev in friends:
         pl.semaphore_signal(barrier, inc=1, device_id=dev, device_id_type=MESH)
@@ -133,15 +133,16 @@
     WR[0:experts, :] = wrt[...]
     for s in range(4):
         for i in range(2):
-            U[s, i, sp:, :] = jnp.zeros((LP - sp, width), BF)
-            G[s, i, sp:, :] = jnp.zeros((LP - sp, width), BF)
-
-    uP = [rc("uP", i, U.at[0, i, top], U.at[1, i, top], to_p) for i in range(2)]
-    uO = [rc("uO", i, U.at[0, i, top], U.at[2, i, top], to_o) for i in range(2)]
-    uF = [rc("uF", i, U.at[2, i, top], U.at[3, i, top], to_p) for i in range(2)]
-    gP = [rc("gP", i, G.at[0, i, top], G.at[1, i, top], to_p) for i in range(2)]
-    gO = [rc("gO", i, G.at[0, i, top], G.at[2, i, top], to_o) for i in range(2)]
-    gF = [rc("gF", i, G.at[2, i, top], G.at[3, i, top], to_p) for i in range(2)]
+            first = sent.size if s else sp
+            U[s, i, first:, :] = jnp.zeros((LP - first, width), BF)
+            G[s, i, first:, :] = jnp.zeros((LP - first, width), BF)
+
+    uP = [rc("uP", i, U.at[0, i, sent], U.at[1, i, sent], to_p) for i in range(2)]
+    uO = [rc("uO", i, U.at[0, i, sent], U.at[2, i, sent], to_o) for i in range(2)]
+    uF = [rc("uF", i, U.at[2, i, sent], U.at[3, i, sent], to_p) for i in range(2)]
+    gP = [rc("gP", i, G.at[0, i, sent], G.at[1, i, sent], to_p) for i in range(2)]
+    gO = [rc("gO", i, G.at[0, i, sent], G.at[2, i, sent], to_o) for i in range(2)]
+    gF = [rc("gF", i, G.at[2, i, sent], G.at[3, i, sent], to_p) for i in range(2)]
     sP = rc("sP", 0, SL.at[0], SL.at[1], to_p)
     sO = rc("sO", 0, SL.at[0], SL.at[2], to_o)
     sF = rc("sF", 0, SL.at[2], SL.at[3], to_p)
@@ -379,20 +380,21 @@
 
             @pl.when(is_end)
             def _():
-                for t in range(2):
+                for t in range(1 if j == 3 else 2):
                     iq(j, t).start()
                     if j == 0:
                         jq(t).start()
 
-            iz(j).start()
+            if j < 3:
+                iz(j).start()
             if j == 0:
                 jz.start()
 
-    def pass_i(j):
+    def pass_i(j, which=(0, 1)):
         with sc("pass_i%d" % j):
             @pl.when(is_mid)
             def _():
-                for t in range(2):
+                for t in which:
                     at = (far, near)[t]
                     iq(j, t).wait_recv()
                     if j == 0:
@@ -771,21 +773,28 @@
         SM[at, :] = (SM[at, :].astype(F32) + SMx[2].astype(F32)).astype(BF)
         mX.start()
     stage_r1(3)
+
+    @pl.when(is_end)
+    def _():
+        iq(3, 1).start()
+
+    pass_i(3, (0,))
     stage_r1(0)
-    pass_i(3)
     stage_r2(3)
+    pass_i(3, (1,))
     stage_r1(1)
     stage_r2(0)
     stage_r1(2)
-    stage_r2(1)
-    stage_r3(3)
-    stage_r2(2)
-    stage_r3(0)
+    iz(3).start()
     with sc("small_z"):
         mX.wait_recv()
         SMx[3] = (SM[small(ep), :].astype(F32) + SMx[3].astype(F32)).astype(BF)
         for cp in mZ:
             cp.start()
+    stage_r2(1)
+    stage_r3(3)
+    stage_r2(2)
+    stage_r3(0)
     stage_r3(1)
     stage_r3(2)
     for j in range(4):
@@ -859,7 +868,6 @@
     pads = ((0, 0), (0, sp - seq), (0, 0))
     gl = jnp.pad(cot, pads)
     xb = jnp.pad(tokens, pads)
-    gains = jnp.stack([g1, b1, g2, b2])
     sds = jax.ShapeDtypeStruct
     vm = pl.BlockSpec(memory_space=pltpu.VMEM)
     anys = pl.BlockSpec(memory_space=pl.ANY)
@@ -874,7 +882,7 @@
             sds((width, f // 8), BF), sds((width // 8, f), BF), sds((shard, 4 * width), BF),
             sds((2 * sp, 4 * width), BF), sds((2 * sp, width), BF), sds((2 * sp, width), BF),
         ),
-        in_specs=[pl.BlockSpec(memory_space=pltpu.SMEM)] + [vm] * 3 + [anys] * 6,
+        in_specs=[pl.BlockSpec(memory_space=pltpu.SMEM)] + [vm] * 6 + [anys] * 6,
         out_specs=[vm] * 3 + [anys] * 6,
         scratch_shapes=[
             b(4, 2, LP, width), b(4, 2, LP, width), g(4, 2, 8, LP), b(128, width), b(width, f), b(f, width),
@@ -891,7 +899,7 @@
         ],
         compiler_params=pltpu.CompilerParams(
             collective_id=0, has_side_effects=True, vmem_limit_bytes=67043328),
-    )(live, jnp.transpose(routes, (0, 2, 1)), gains, jnp.transpose(wr), xb, gl, w_in, w_out, wqkv, wo)
+    )(live, jnp.transpose(routes, (0, 2, 1)), g1, b1, g2, b2, jnp.transpose(wr), xb, gl, w_in, w_out, wqkv, wo)
     return (
         bo[:, :seq], gt[:, :seq], sm[4], sm[5], sg[:, :3 * width].astype(F32), sg[:, 3 * width:].astype(F32),
         sm[6], sm[7], jnp.transpose(sm[:n_ep]), wi.astype(F32)[None], jnp.transpose(wo_t).astype(F32)[None],

time: 203 us -> 196 us (0.966)
  Pallas kernels: 182 us -> 178 us
  local copies, waits for them, and re-layouts: 12.7 us -> 9.9 us
    pallas_call x1, Pallas kernels: 182 us -> 178 us  [fast_body(): pl.pallas_call(functools.partial(layer_kernel, n_ep, seq), name='layer',...]
    another operation x4 -> x0, local copies, waits for them, and re-layouts: 2.76 us -> none  [fast_body(): gains = jnp.stack([g1, b1, g2, b2])]
where the time goes in v3:
time: 196 us; the launch traced here: 193 us
  Pallas kernels  178 us (91%)
  local copies, waits for them, and re-layouts  9.9 us (5%)
  other arithmetic  3.37 us (2%)
    pallas_call x1, Pallas kernels, fast_body(): pl.pallas_call(functools.partial(layer_kernel, n_ep, seq), name='layer',...  178 us
    unnamed x17, local copies, waits for them, and re-layouts  5.69 us

profile of v3, /device:TPU:0, one launch (start us, length us, event | category | flops | bytes accessed | tf_op | source)
XLA Modules:
  0.0 192.9 jit_solution(7472513803559551212)
XLA Ops:
  1.3 0.0 copy-start.2
  1.3 1.2 copy.24
  2.5 0.9 pad.7.xb
  3.4 0.0 copy-done.2
  3.4 0.1 copy.25
  3.4 0.9 pad.8.gl
  4.3 177.8 %layer.1 = (bf16[2,208,768]{2,1,0:T(8,128)(2,1)}, f32[2,208,768]{2,1,0:T(8,128)}, f32[8,192]{1,0:T(8,128)}, bf16[768,384]{1,0:T(8,128)(2,1)}, bf16[96,3072]{1,0:...) custom-call(s32[1]{0:T(128)S(6)} %copy.29.live, ...), custom_call_target="tpu_custom_call" | custom-call | tf_op jit(solution)/shard_map/layer/pallas_call | solution.py:877
  182.2 0.0 copy-start.5
  182.2 0.0 copy-start.1
  182.2 1.2 slice.27
  183.4 1.3 copy.26
  184.7 0.0 copy-done.5
  184.7 0.6 slice_bitcast_fusion
  185.3 0.6 fusion
  185.9 0.0 copy-done.1
  185.9 0.9 slice_convert_fusion.1
  186.7 0.0 copy-start.4
  186.7 1.3 slice_convert_fusion
  188.0 0.0 copy-done.4
  188.0 0.0 copy-start.3
  188.0 1.1 bitcast_convert_fusion
  189.2 0.1 copy-done.3
  189.2 0.1 convert_bitcast_fusion
  189.3 0.0 copy-start
  189.3 1.4 copy.28
  190.7 0.0 copy-done
  190.7 0.1 slice.28
  190.8 1.6 copy.27
Async XLA Ops:
  1.3 2.1 %copy-start.2 = (bf16[2,197,768]{2,0,1:T(2,128)(2,1)S(1)}, bf16[2,197,768]{2,0,1:T(2,128)(2,1)}, u32[]{:S(2)}) copy-start(bf16[2,197,768]{2,0,1:T(2,128)(2,1)} %param.25) | copy-start | bytes 1815556
  182.2 2.5 %copy-start.5 = (f32[8,192]{1,0:T(8,128)S(1)}, f32[8,192]{1,0:T(8,128)}, u32[]{:S(2)}) copy-start(f32[8,192]{1,0:T(8,128)} %get-tuple-element.19) | copy-start | bytes 18436
  182.2 3.7 %copy-start.1 = (bf16[192,3072]{1,0:T(8,128)(2,1)S(1)}, bf16[192,3072]{1,0:T(8,128)(2,1)}, u32[]{:S(2)}) copy-start(bf16[192,3072]{1,0:T(8,128)(2,1)} %get-tuple-element.20) | copy-start | bytes 3538948
  186.7 1.3 copy-start.4
  188.0 1.2 copy-start.3
  189.3 1.4 copy-start

commit v4 on v3

--- a/solution.py
+++ b/solution.py
@@ -68,10 +68,10 @@
 
 def layer_kernel(
     experts, seq, live, routes, g1, b1, g2, b2, wrt, xb, gl, w_in, w_out, wqkv, wo,
-    bo_o, DH, sm_o, wo_o, wi_o, sg_o, qa_h, c_h, u_h,
+    bo_o, gt_o, sm_o, wo_o, wi_o, sg_o, qa_h, c_h, u_h,
     U, G, SL, WR, WI, WO, M, D, X, GE, DT,
     GOs, GOk, GOx, GOz, GIs, GIk, GIx, GIz, GJ,
-    H, LS, GD, RP, RD, RO, EP, ED, EO, ES, YP, YD, YO, SM, SMx,
+    H, DH, LS, GD, RP, RD, RO, EP, ED, EO, ES, YP, YD, YO, SM, SMx, SZ,
     ssem, rsem, lsem, free, credit,
 ):
     f, width = WO.shape
@@ -421,6 +421,10 @@
     GD[:, 1:2] = jnp.zeros((GD.shape[0], 1), F32)
 
     def expert_back(n, carry):
+        @pl.when(n == tiles // 2)
+        def _():
+            take_o(0)
+
         cols = pl.ds(pl.multiple_of(n * tile, tile), tile)
         for first in (0, half_rows):
             rs = slice(first, first + half_rows)
@@ -430,10 +434,7 @@
         return carry
 
     with sc("expert_back"):
-        lax.fori_loop(0, tiles // 2, expert_back, 0)
-    take_o(0)
-    with sc("expert_back"):
-        lax.fori_loop(tiles // 2, tiles, expert_back, 0)
+        lax.fori_loop(0, tiles, expert_back, 0)
 
     dP = [rc("dP", i, U.at[1, i, top], RP.at[i], to_p) for i in range(2)]
     dD = [rc("dD", i, U.at[3, i, top], RD.at[i], to_p) for i in range(2)]
@@ -660,12 +661,14 @@
                 total = WI[own_rows(), half(b, x)].astype(F32) + rest(4, b, 1)[...].astype(F32)
                 rest(0, b, 0)[...] = total.astype(BF)
                 cp_r3(b).start()
-
+                cp_ax(b).start()
+
+    def stage_r4(b):
+        with sc("stage_r4_%d" % b):
             @pl.when(is_end)
             def _():
                 cp_r3(b).wait_recv()
-
-            cp_ax(b).start()
+                cp_ax(b).start()
 
     with sc("attn_out_grads"):
         X[half_rows:half_rows + rows, :] = dot_nt(GE[0:rows, :], WO[3 * width:, :]).astype(BF)
@@ -675,6 +678,12 @@
     stage_c(3)
 
     def pair_back(h, carry):
+        @pl.when(h == width // 256)
+        def _():
+            stage_y(3)
+            pass_i(0)
+            take_o(3)
+
         def cols(n):
             return pl.ds(pl.multiple_of(h * 128 + n * width, 128), 128)
 
@@ -698,13 +707,8 @@
                 M[r1, cols(n + 1)] = jnp.where(low, parts[0][n], parts[1][n]).astype(BF)
         return carry
 
-    with sc("attention_back_a"):
-        lax.fori_loop(0, width // 256, pair_back, 0)
-    stage_y(3)
-    pass_i(0)
-    take_o(3)
-    with sc("attention_back_b"):
-        lax.fori_loop(width // 256, width // 128, pair_back, 0)
+    with sc("attention_back"):
+        lax.fori_loop(0, width // 128, pair_back, 0)
     for n in range(3):
         with sc("qkv_grads"):
             grads = M[rows:2 * rows, (n + 1) * width:(n + 2) * width]
@@ -734,7 +738,7 @@
     mC = [rc("mC", i, SM.at[small(i * 2 + 1 - core)], SMx.at[i], to_p) for i in range(2)]
     mY = rc("mY", 0, SM.at[small((1 - y) * 2 + core)], SMx.at[2], to_o)
     mX = rc("mX", 0, SM.at[small(ep)], SMx.at[3], to_x)
-    mZ = [rc("mZ", k - 1, SMx.at[3], SMx.at[3 + k], to_z[k]) for k in range(1, 4)]
+    mZ = [rc("mZ", k - 1, SZ.at[0], SZ.at[k], to_z[k]) for k in range(1, 4)]
     for cp in mC:
         cp.start()
     for b in range(3):
@@ -763,6 +767,9 @@
     pass_i(1)
     take_i(2)
     stage_x(0)
+    with sc("rows_out"):
+        for i in range(2):
+            gt_o[:, i, :] = DH[i, :seq, :]
     pass_i(2)
     stage_x(1)
     take_i(3)
@@ -784,19 +791,32 @@
     pass_i(3, (1,))
     stage_r1(1)
     stage_r2(0)
+    stage_r3(3)
     stage_r1(2)
-    iz(3).start()
+
+    @pl.when(is_end)
+    def _():
+        iz(3).start()
+
+    stage_r2(1)
+    stage_r3(0)
+    stage_r2(2)
     with sc("small_z"):
         mX.wait_recv()
-        SMx[3] = (SM[small(ep), :].astype(F32) + SMx[3].astype(F32)).astype(BF)
+        total = jnp.transpose(SM[small(ep), :].astype(F32) + SMx[3].astype(F32))
+        SZ[0, :, :shard] = total[0:8, :]
+        SZ[0, :, shard:] = jnp.zeros((8, LP - shard), F32)
         for cp in mZ:
             cp.start()
-    stage_r2(1)
-    stage_r3(3)
-    stage_r2(2)
-    stage_r3(0)
     stage_r3(1)
     stage_r3(2)
+
+    @pl.when(is_mid)
+    def _():
+        iz(3).start()
+
+    for b in (3, 0, 1, 2):
+        stage_r4(b)
     for j in range(4):
         with sc("i_sum%d" % j):
             iz(j).wait_recv()
@@ -811,8 +831,7 @@
     with sc("small_sum"):
         for cp in mZ:
             cp.wait_recv()
-        total = SMx[3].astype(F32) + SMx[4].astype(F32) + SMx[5].astype(F32) + SMx[6].astype(F32)
-        sm_o[...] = jnp.transpose(total)[0:8, :]
+        sm_o[...] = (SZ[0] + SZ[1] + SZ[2] + SZ[3])[:, :shard]
     for b in (3, 0, 1, 2):
         with sc("wait_ax"):
             cp_ax(b).wait_recv()
@@ -878,7 +897,7 @@
         functools.partial(layer_kernel, n_ep, seq),
         name="layer",
         out_shape=(
-            sds((slots, sp, width), BF), sds((slots, sp, width), F32), sds((8, shard), F32),
+            sds((slots, sp, width), BF), sds((seq, slots, width), F32), sds((8, shard), F32),
             sds((width, f // 8), BF), sds((width // 8, f), BF), sds((shard, 4 * width), BF),
             sds((2 * sp, 4 * width), BF), sds((2 * sp, width), BF), sds((2 * sp, width), BF),
         ),
@@ -890,10 +909,10 @@
             b(4, width, f // 8), b(4, width, f // 8), b(4, width, f // 8), b(2, width, f // 8),
             b(4, 4, width // 8, width), b(4, 4, width // 8, width), b(4, 4, width // 8, width),
             b(2, 4, width // 8, width), b(4, width // 8, width),
-            g(slots, sp, width), g(slots, sp, 128), g(cap, 2),
+            g(slots, sp, width), g(slots, sp, width), g(slots, sp, 128), g(cap, 2),
             b(2, sp, width), b(2, sp, width), b(2, sp, width),
             b(2, LP, 128), b(2, LP, 128), b(2, LP, 128), b(4, 2, LP, 128),
-            b(2, sp, width), b(2, sp, width), b(2, sp, width), b(width, 128), b(7, shard, 128),
+            b(2, sp, width), b(2, sp, width), b(2, sp, width), b(width, 128), b(4, shard, 128), g(4, 8, LP),
             pltpu.SemaphoreType.DMA((N_COPIES,)), pltpu.SemaphoreType.DMA((N_COPIES,)),
             pltpu.SemaphoreType.DMA((14,)), pltpu.SemaphoreType.REGULAR, pltpu.SemaphoreType.REGULAR((2,)),
         ],
@@ -901,7 +920,7 @@
             collective_id=0, has_side_effects=True, vmem_limit_bytes=67043328),
     )(live, jnp.transpose(routes, (0, 2, 1)), g1, b1, g2, b2, jnp.transpose(wr), xb, gl, w_in, w_out, wqkv, wo)
     return (
-        bo[:, :seq], gt[:, :seq], sm[4], sm[5], sg[:, :3 * width].astype(F32), sg[:, 3 * width:].astype(F32),
+        bo[:, :seq], jnp.transpose(gt, (1, 0, 2)), sm[4], sm[5], sg[:, :3 * width].astype(F32), sg[:, 3 * width:].astype(F32),
         sm[6], sm[7], jnp.transpose(sm[:n_ep]), wi.astype(F32)[None], jnp.transpose(wo_t).astype(F32)[None],
     )
 

time: 196 us -> 188 us (0.959); the launches traced: 193 us -> 188 us
  Pallas kernels: 178 us -> 174 us
    pallas_call x1, Pallas kernels: 178 us -> 174 us  [fast_body(): pl.pallas_call(functools.partial(layer_kernel, n_ep, seq), name='layer',...]
where the time goes in v4:
time: 188 us
  Pallas kernels  174 us (93%)
  local copies, waits for them, and re-layouts  9.2 us (5%)
  other arithmetic  3.37 us (2%)
    pallas_call x1, Pallas kernels, fast_body(): pl.pallas_call(functools.partial(layer_kernel, n_ep, seq), name='layer',...  174 us
    unnamed x17, local copies, waits for them, and re-layouts  5.06 us

profile of v4, /device:TPU:0, one launch (start us, length us, event | category | flops | bytes accessed | tf_op | source)
XLA Modules:
  0.0 188.1 jit_solution(18332540859147754126)
XLA Ops:
  1.3 0.0 copy-start.2
  1.3 1.2 copy.24
  2.5 0.9 pad.7.xb
  3.4 0.0 copy-done.2
  3.4 0.1 copy.25
  3.4 0.9 pad.8.gl
  4.3 174.2 %layer.1 = (bf16[2,208,768]{2,1,0:T(8,128)(2,1)}, f32[197,2,768]{2,1,0:T(2,128)}, f32[8,192]{1,0:T(8,128)}, bf16[768,384]{1,0:T(8,128)(2,1)}, bf16[96,3072]{1,0:...) custom-call(s32[1]{0:T(128)S(6)} %copy.29.live, ...), custom_call_target="tpu_custom_call" | custom-call | tf_op jit(solution)/shard_map/layer/pallas_call | solution.py:896
  178.5 0.0 copy-start.5
  178.5 0.0 copy-start.1
  178.5 1.2 slice.24
  179.7 1.3 copy.26
  181.0 0.0 copy-done.5
  181.0 0.6 slice_bitcast_fusion
  181.6 0.6 fusion
  182.2 0.0 copy-done.1
  182.2 0.9 slice_convert_fusion.1
  183.0 0.0 copy-start.4
  183.0 1.3 slice_convert_fusion
  184.4 0.0 copy-done.4
  184.4 0.0 copy-start.3
  184.4 1.1 bitcast_convert_fusion
  185.5 0.1 copy-done.3
  185.6 0.1 convert_bitcast_fusion
  185.7 0.0 copy-start
  185.7 1.4 copy.27
  187.1 0.0 copy-done
  187.1 1.0 copy.30
Async XLA Ops:
  1.3 2.1 %copy-start.2 = (bf16[2,197,768]{2,0,1:T(2,128)(2,1)S(1)}, bf16[2,197,768]{2,0,1:T(2,128)(2,1)}, u32[]{:S(2)}) copy-start(bf16[2,197,768]{2,0,1:T(2,128)(2,1)} %param.25) | copy-start | bytes 1815556
  178.5 2.5 %copy-start.5 = (f32[8,192]{1,0:T(8,128)S(1)}, f32[8,192]{1,0:T(8,128)}, u32[]{:S(2)}) copy-start(f32[8,192]{1,0:T(8,128)} %get-tuple-element.19) | copy-start | bytes 18436
  178.5 3.7 %copy-start.1 = (bf16[192,3072]{1,0:T(8,128)(2,1)S(1)}, bf16[192,3072]{1,0:T(8,128)(2,1)}, u32[]{:S(2)}) copy-start(bf16[192,3072]{1,0:T(8,128)(2,1)} %get-tuple-element.20) | copy-start | bytes 3538948
  183.0 1.3 copy-start.4
  184.4 1.2 copy-start.3
  185.7 1.4 copy-start
